TPU v7x, 16 devices: a 4x2x1 block of a 4x4x8 slice. The times are simulated.
16 devices in a mesh: dp: 2 (over y, z), tp: 8 (over x, core).
Axes of the slice: x: 4, y: 2, z: 1, core: 2. Of those that a mesh axis runs over, the one named last changes fastest.
The devices are a block of a 4x4x8 slice.
Arguments:
- act_in: bfloat16 [16, 1024, 2560], P('dp'), parts along dimension 0
- ln_gain: float32 [2, 2560], replicated
- ln_bias: float32 [2, 2560], replicated
- w_qkv: bfloat16 [2, 2560, 32, 240], P(None, None, 'tp')
- w_out: bfloat16 [2, 2560, 2560], P(None, 'tp')
- w_up: bfloat16 [2, 2560, 10240], P(None, None, 'tp')
- w_down: bfloat16 [2, 10240, 2560], P(None, 'tp')
Outputs:
- output: bfloat16 [16, 1024, 2560], P('dp'), parts along dimension 0
There are 2 independent parts. A program takes and returns all parts, laid end to end along the dimension named above; an argument that names none is the same for every part.
All inputs are finite; a program needn't handle non-finite values.
Results may differ from a plain program's by a relative error of at most 0.0174878.
Values are sent between devices in bfloat16 or wider.
A program may use at most 768 MiB of HBM per device.

v0:
```python
import jax
import jax.numpy as jnp
from jax import lax
from jax.sharding import PartitionSpec as P

LN_EPS = 1e-5
ROPE_BASE = 10000.0


def layer_norm(hidden, gain, bias):
    hidden_f = hidden.astype(jnp.float32)
    row_mean = jnp.mean(hidden_f, axis=-1, keepdims=True)
    centered = hidden_f - row_mean
    row_var = jnp.mean(centered * centered, axis=-1, keepdims=True)
    return (centered * lax.rsqrt(row_var + LN_EPS) * gain + bias).astype(jnp.bfloat16)


def rope_tables(seq_len, head_dim):
    half_dim = head_dim // 2
    inv_freq = ROPE_BASE ** (-2.0 * jnp.arange(half_dim, dtype=jnp.float32) / head_dim)
    angles = jnp.arange(seq_len, dtype=jnp.float32)[:, None] * inv_freq[None, :]
    return jnp.cos(angles), jnp.sin(angles)


def apply_rope(proj, cos_tab, sin_tab):
    half_dim = proj.shape[-1] // 2
    first = proj[..., :half_dim]
    second = proj[..., half_dim:]
    return jnp.concatenate([first * cos_tab - second * sin_tab, second * cos_tab + first * sin_tab], axis=-1)


def layer_partial(hidden, gain, bias, w_qkv, w_out, w_up, w_down):
    batch, seq_len, d_model = hidden.shape
    groups = w_qkv.shape[1]
    attn_width = w_out.shape[0]
    head_dim = (w_qkv.shape[2] - attn_width // groups) // 2
    group_heads = attn_width // (groups * head_dim)
    normed = layer_norm(hidden, gain, bias)
    qkv_proj = jnp.einsum("bsd,dgc->bsgc", normed, w_qkv, preferred_element_type=jnp.float32)
    qkv_proj = qkv_proj.reshape(batch, seq_len, groups, group_heads + 2, head_dim)
    cos_tab, sin_tab = rope_tables(seq_len, head_dim)
    query = apply_rope(qkv_proj[:, :, :, :group_heads], cos_tab[None, :, None, None, :], sin_tab[None, :, None, None, :]).astype(jnp.bfloat16)
    keys = apply_rope(qkv_proj[:, :, :, group_heads], cos_tab[None, :, None, :], sin_tab[None, :, None, :]).astype(jnp.bfloat16)
    values = qkv_proj[:, :, :, group_heads + 1].astype(jnp.bfloat16)
    scores = jnp.einsum("bsgrd,btgd->bgrst", query, keys, preferred_element_type=jnp.float32) * (head_dim ** -0.5)
    positions = jnp.arange(seq_len)
    allowed = positions[:, None] >= positions[None, :]
    scores = jnp.where(allowed, scores, -1e30)
    attn_probs = jax.nn.softmax(scores, axis=-1).astype(jnp.bfloat16)
    context = jnp.einsum("bgrst,btgd->bgrsd", attn_probs, values, preferred_element_type=jnp.float32).astype(jnp.bfloat16)
    out_heads = w_out.reshape(groups, group_heads, head_dim, d_model)
    attn_part = jnp.einsum("bgrsd,grde->bse", context, out_heads, preferred_element_type=jnp.float32)
    up_proj = jnp.einsum("bsd,df->bsf", normed, w_up, preferred_element_type=jnp.float32)
    gelu_out = jax.nn.gelu(up_proj, approximate=False).astype(jnp.bfloat16)
    mlp_part = jnp.einsum("bsf,fe->bse", gelu_out, w_down, preferred_element_type=jnp.float32)
    return attn_part + mlp_part


def solution(mesh):
    def shard_body(act_in, ln_gain, ln_bias, w_qkv, w_out, w_up, w_down):
        hidden = act_in
        for layer_idx in range(ln_gain.shape[0]):
            local_sum = layer_partial(hidden, ln_gain[layer_idx], ln_bias[layer_idx], w_qkv[layer_idx], w_out[layer_idx], w_up[layer_idx], w_down[layer_idx]).astype(jnp.bfloat16)
            reduced = lax.psum(local_sum, "tp")
            hidden = (hidden.astype(jnp.float32) + reduced.astype(jnp.float32)).astype(jnp.bfloat16)
        return hidden

    return jax.shard_map(shard_body, mesh=mesh, in_specs=(P("dp", None, None), P(None, None), P(None, None), P(None, None, "tp", None), P(None, "tp", None), P(None, None, "tp"), P(None, "tp", None)), out_specs=P("dp", None, None), check_vma=False)
```

profile of v0, /device:TPU:113, one launch (start us, length us, event | category | flops | bytes accessed | tf_op | source)
XLA Modules:
  0.0 1944.5 jit_solution(2906867723270431644)
XLA Ops:
  6.5 0.0 all-reduce.3.cloned.1.call-start
  6.6 1.3 iota_compare_fusion
  7.8 8.4 fusion.252
  16.2 14.1 convert_reduce_fusion.1
  30.3 0.0 copy-start.10
  30.3 0.0 slice-start.3
  30.3 18.4 fusion.12
  48.8 0.0 copy-start.12
  48.8 0.7 fusion.178
  49.5 0.0 copy-done.14
  49.5 0.0 copy-done.15
  49.5 0.0 copy-start.2
  49.5 0.0 copy-start.5
  49.5 0.7 slice_reduce_fusion
  50.2 0.0 slice-done.2
  50.2 0.0 slice-done.3
  50.2 49.6 %fusion.32 = f32[8,1024,4,3,80]{1,4,3,2,0:T(8,128)} fusion(bf16[4,3,80,2560,1]{3,2,1,0,4:T(8,128)(2,1)S(1)} %bitcast.228, bf16[8,1024,2560]{2,1,0:T(8,128)(2,1)} %param.7, f32[2560]{0:T(1024)S(1)} %get-tuple-element.12, f32[2560]{0:T(1024)S(1)} %get-tuple-element.33, f32[8,1024]{1,0:T(8,128)S(1)} %add_rsqrt_fusion.1, f32[8,1024]{1,0:T(8,128)S(1)} %broadcast_multiply_fusion.1), kind=kOutput, calls=%fused_computation.57 | convolution fusion | flops 40391147520 | bytes 78401536 | tf_op jit(solution)/shard_map/bsd,dgc->bsgc/dot_general | solution.py:39
  99.9 0.0 copy-done.10
  99.9 0.0 copy-done.12
  99.9 0.0 copy-done.18
  99.9 0.0 copy-done.20
  99.9 0.0 copy-start
  99.9 7.1 fusion.176
  107.0 7.2 fusion.175
  114.1 5.1 slice_bitcast_fusion.1
  119.2 3.9 fusion.253
  123.1 0.0 copy-done.2
  123.1 0.0 copy-done.5
  123.1 3.4 subtract_convert_fusion.2
  126.5 0.0 copy-done
  126.5 48.8 %fusion.2 = (f32[8,4,1024]{2,1,0:T(4,128)S(1)}, f32[8,4,1024,1024]{3,2,1,0:T(8,128)}) fusion(pred[1024,1024]{0,1:T(8,128)(4,1)S(1)} %copy-done, bf16[8,1024,4,40]{1,3,2,0:T(8,128)(2,1)} %fusion.176, bf16[8,1024,4,40]{1,3,2,0:T(8,128)(2,1)} %fusion.175, bf16[8,1024,4,40]{1,3,2,0:T(8,128)(2,1)} %get-tuple-element.20, ...), kind=kOutput, calls=%fused_computation.14 | convolution fusion | flops 5490311168 | bytes 145883136 | tf_op jit(solution)/shard_map/bsgrd,btgd->bgrst/dot_general | solution.py:45
  175.3 41.2 %fusion = f32[8,4,1024]{2,1,0:T(4,128)S(1)} fusion(f32[8,4,1024,1024]{3,2,1,0:T(8,128)} %get-tuple-element.28, f32[8,4,1024]{2,1,0:T(4,128)S(1)} %get-tuple-element.27, pred[1024,1024]{0,1:T(8,128)(4,1)S(1)} %copy-done), kind=kLoop, calls=%fused_computation.12 | loop fusion | flops 134184960 | bytes 135528448 | tf_op jit(solution)/shard_map/reduce_sum | solution.py:49
  216.5 0.0 copy-start.11
  216.5 0.0 copy-start.13
  216.5 0.0 copy-start.19
  216.5 0.0 copy-start.21
  216.5 50.7 %fusion.283 = bf16[8,4,1024,80]{2,3,1,0:T(8,128)(2,1)} fusion(f32[8,4,1024]{2,1,0:T(4,128)S(1)} %fusion, f32[8,4,1024]{2,1,0:T(4,128)S(1)} %get-tuple-element.27, f32[8,4,1024,1024]{3,2,1,0:T(8,128)} %get-tuple-element.28, pred[1024,1024]{0,1:T(8,128)(4,1)S(1)} %copy-done, f32[8,1024,4,3,80]{1,4,3,2,0:T(8,128)} %fusion.32), kind=kOutput, calls=%fused_computation.201.clone | convolution fusion | flops 5539102720 | bytes 146014208 | tf_op jit(solution)/shard_map/bgrst,btgd->bgrsd/dot_general | solution.py:50
  267.2 0.0 copy-done.11
  267.2 0.0 copy-done.19
  267.2 77.9 %fusion.118 = (u8[1024,1280]{1,0:T(8,128)(4,1)S(1)}, u8[1024,1280]{1,0:T(8,128)(4,1)}, f32[8,1024,1280]{2,1,0:T(8,128)}) fusion(bf16[2,2560,1280]{2,1,0:T(8,128)(2,1)} %param.12, bf16[8,1024,2560]{2,1,0:T(8,128)(2,1)} %param.7, f32[2560]{0:T(1024)S(1)} %copy-done.19, f32[2560]{0:T(1024)S(1)} %copy-done.21, f32[8,1024]{1,0:T(8,128)S(1)} %copy-done.13, ...), kind=kOutput, calls=%fused_computation.155 | convolution fusion | flops 53946613760 | bytes 93147136 | tf_op jit(solution)/shard_map/bsd,df->bsf/dot_general | solution.py:53
  345.1 34.2 %fusion.163 = f32[8,1024,2560,1]{2,1,3,0:T(8,128)} fusion(bf16[4,80,2560,1]{2,1,0,3:T(8,128)(2,1)S(1)} %bitcast.230, bf16[8,4,1024,80]{2,3,1,0:T(8,128)(2,1)} %fusion.283), kind=kOutput, calls=%fused_computation.200 | convolution fusion | flops 13421772800 | bytes 90767360 | tf_op jit(solution)/shard_map/bgrsd,grde->bse/dot_general | solution.py:52
  379.3 153.0 %fusion.19 = bf16[8,1024,2560]{2,1,0:T(8,128)(2,1)} fusion(f32[8,1024,2560,1]{2,1,3,0:T(8,128)} %fusion.163, f32[8,1024,1280]{2,1,0:T(8,128)} %get-tuple-element.29, bf16[2,1280,2560]{2,1,0:T(8,128)(2,1)} %param.13, u8[1024,1280]{1,0:T(8,128)(4,1)} %get-tuple-element.8, u8[1024,1280]{1,0:T(8,128)(4,1)S(1)} %get-tuple-element.7), kind=kOutput, calls=%fused_computation.33 | convolution fusion | flops 54463037440 | bytes 176947200 | tf_op jit(solution)/shard_map/bsf,fe->bse/dot_general | solution.py:55
  532.3 0.1 all-reduce.3.cloned.1.call-update
  532.4 0.1 all-reduce.5.cloned.1.call-start
  532.5 413.7 %all-reduce.3.cloned.1.call-done = bf16[8,1024,2560]{2,1,0:T(8,128)(2,1)} async-done(((bf16[8,1024,2560]{2,1,0:T(8,128)(2,1)}), bf16[8,1024,2560]{2,1,0:T(8,128)(2,1)}) %all-reduce.3.cloned.1.call-update) | async-done | bytes 41943056 | tf_op jit(solution)/shard_map/psum | solution.py:64
  946.1 41.4 %convert_reduce_fusion = (f32[8,1024]{1,0:T(8,128)S(1)}, bf16[8,1024,2560]{2,1,0:T(8,128)(2,1)}) fusion(bf16[8,1024,2560]{2,1,0:T(8,128)(2,1)} %all-reduce.3.cloned.1.call-done, bf16[8,1024,2560]{2,1,0:T(8,128)(2,1)} %param.7), kind=kLoop, calls=%fused_computation.8 | loop fusion | flops 125820928 | bytes 125861888 | tf_op jit(solution)/shard_map/reduce_sum | solution.py:12
  987.5 0.0 slice-start.1
  987.5 18.5 fusion.8
  1006.1 49.8 %fusion.30 = f32[8,1024,4,3,80]{1,4,3,2,0:T(8,128)} fusion(bf16[4,3,80,2560,1]{3,2,1,0,4:T(8,128)(2,1)S(1)} %bitcast.225, bf16[8,1024,2560]{2,1,0:T(8,128)(2,1)} %get-tuple-element.14, f32[2560]{0:T(1024)S(1)} %copy-done.16, f32[2560]{0:T(1024)S(1)} %copy-done.17, f32[8,1024]{1,0:T(8,128)S(1)} %add_rsqrt_fusion, f32[8,1024]{1,0:T(8,128)S(1)} %broadcast_multiply_fusion), kind=kOutput, calls=%fused_computation.55 | convolution fusion | flops 40391147520 | bytes 78401536 | tf_op jit(solution)/shard_map/bsd,dgc->bsgc/dot_general | solution.py:39
  1055.9 0.0 copy-done.6
  1055.9 6.6 fusion.173
  1062.5 10.2 slice_bitcast_fusion
  1072.7 77.9 %fusion.119 = (u8[1024,1280]{1,0:T(8,128)(4,1)}, u8[1024,1280]{1,0:T(8,128)(4,1)}, f32[8,1024,1280]{2,1,0:T(8,128)}) fusion(bf16[2,2560,1280]{2,1,0:T(8,128)(2,1)} %param.12, bf16[8,1024,2560]{2,1,0:T(8,128)(2,1)} %get-tuple-element.14, f32[2560]{0:T(1024)S(1)} %copy-done.16, f32[2560]{0:T(1024)S(1)} %copy-done.17, f32[8,1024]{1,0:T(8,128)S(1)} %add_rsqrt_fusion, ...), kind=kOutput, calls=%fused_computation.156 | convolution fusion | flops 53946613760 | bytes 93147136 | tf_op jit(solution)/shard_map/bsd,df->bsf/dot_general | solution.py:53
  1150.7 0.0 copy-done.4
  1150.7 6.5 subtract_convert_fusion.1
  1157.2 48.6 %fusion.3 = (f32[8,4,1024]{2,1,0:T(4,128)S(1)}, f32[8,4,1024,1024]{3,2,1,0:T(8,128)}) fusion(pred[1024,1024]{0,1:T(8,128)(4,1)S(1)} %copy-done.1, bf16[8,1024,4,40]{1,3,2,0:T(8,128)(2,1)} %get-tuple-element.16, bf16[8,1024,4,40]{1,3,2,0:T(8,128)(2,1)} %get-tuple-element.15, bf16[8,1024,4,40]{1,3,2,0:T(8,128)(2,1)} %get-tuple-element.18, ...), kind=kOutput, calls=%fused_computation.15 | convolution fusion | flops 5490311168 | bytes 145883136 | tf_op jit(solution)/shard_map/bsgrd,btgd->bgrst/dot_general | solution.py:45
  1205.8 41.4 %fusion.1 = f32[8,4,1024]{2,1,0:T(4,128)S(1)} fusion(f32[8,4,1024,1024]{3,2,1,0:T(8,128)} %get-tuple-element.31, f32[8,4,1024]{2,1,0:T(4,128)S(1)} %get-tuple-element.30, pred[1024,1024]{0,1:T(8,128)(4,1)S(1)} %copy-done.1), kind=kLoop, calls=%fused_computation.13 | loop fusion | flops 134184960 | bytes 135528448 | tf_op jit(solution)/shard_map/reduce_sum | solution.py:49
  1247.1 0.0 copy-start.8
  1247.1 50.8 %fusion.279 = bf16[8,4,1024,80]{2,3,1,0:T(8,128)(2,1)} fusion(f32[8,4,1024]{2,1,0:T(4,128)S(1)} %fusion.1, f32[8,4,1024]{2,1,0:T(4,128)S(1)} %get-tuple-element.30, f32[8,4,1024,1024]{3,2,1,0:T(8,128)} %get-tuple-element.31, pred[1024,1024]{0,1:T(8,128)(4,1)S(1)} %copy-done.1, f32[8,1024,4,3,80]{1,4,3,2,0:T(8,128)} %fusion.30), kind=kOutput, calls=%fused_computation.195.clone.1 | convolution fusion | flops 5539102720 | bytes 146014208 | tf_op jit(solution)/shard_map/bgrst,btgd->bgrsd/dot_general | solution.py:50
  1297.9 34.2 %fusion.153 = f32[8,1024,2560,1]{2,1,3,0:T(8,128)} fusion(bf16[4,80,2560,1]{2,1,0,3:T(8,128)(2,1)S(1)} %bitcast.229, bf16[8,4,1024,80]{2,3,1,0:T(8,128)(2,1)} %fusion.279), kind=kOutput, calls=%fused_computation.194 | convolution fusion | flops 13421772800 | bytes 90767360 | tf_op jit(solution)/shard_map/bgrsd,grde->bse/dot_general | solution.py:52
  1332.1 152.9 %fusion.18 = bf16[8,1024,2560]{2,1,0:T(8,128)(2,1)} fusion(f32[8,1024,2560,1]{2,1,3,0:T(8,128)} %fusion.153, f32[8,1024,1280]{2,1,0:T(8,128)} %get-tuple-element.32, bf16[2,1280,2560]{2,1,0:T(8,128)(2,1)} %param.13, u8[1024,1280]{1,0:T(8,128)(4,1)} %get-tuple-element.6, u8[1024,1280]{1,0:T(8,128)(4,1)} %get-tuple-element.5), kind=kOutput, calls=%fused_computation.31 | convolution fusion | flops 54463037440 | bytes 176947200 | tf_op jit(solution)/shard_map/bsf,fe->bse/dot_general | solution.py:55
  1485.0 0.1 all-reduce.5.cloned.1.call-update
  1485.0 410.9 %all-reduce.5.cloned.1.call-done = bf16[8,1024,2560]{2,1,0:T(8,128)(2,1)} async-done(((bf16[8,1024,2560]{2,1,0:T(8,128)(2,1)}), bf16[8,1024,2560]{2,1,0:T(8,128)(2,1)}) %all-reduce.5.cloned.1.call-update) | async-done | bytes 41943056 | tf_op jit(solution)/shard_map/psum | solution.py:64
  1895.9 41.3 %fusion.17 = bf16[8,1024,2560]{2,1,0:T(8,128)(2,1)} fusion(bf16[8,1024,2560]{2,1,0:T(8,128)(2,1)} %get-tuple-element.14, bf16[8,1024,2560]{2,1,0:T(8,128)(2,1)} %all-reduce.5.cloned.1.call-done), kind=kLoop, calls=%fused_computation.29 | loop fusion | flops 83886080 | bytes 125829120 | tf_op jit(solution)/shard_map/convert_element_type | solution.py:65
  (32 shorter events, 0.1 us)
Async XLA Ops:
  6.5 939.6 %all-reduce.3.cloned.1.call-start = ((), (), s32[]{:S(2)}) async-start(), calls=%async_computation | async-start | bytes 83886080 | tf_op jit(solution)/shard_map/psum | solution.py:64
  16.2 33.2 %copy-start.14 = (f32[2,2560]{1,0:T(2,128)S(1)}, f32[2,2560]{1,0:T(2,128)}, u32[]{:S(2)}) copy-start(f32[2,2560]{1,0:T(2,128)} %param.9) | copy-start | bytes 61444
  16.2 33.2 %copy-start.15 = (f32[2,2560]{1,0:T(2,128)S(1)}, f32[2,2560]{1,0:T(2,128)}, u32[]{:S(2)}) copy-start(f32[2,2560]{1,0:T(2,128)} %param.8) | copy-start | bytes 61444
  16.2 34.0 %slice-start.2 = ((s8[4915200]{0:T(1024)(128)(4,1)}), s8[4194304]{0:T(1024)(128)(4,1)S(1)}, s32[]{:S(2)}) async-start(s8[4915200]{0:T(1024)(128)(4,1)} %bitcast.226), calls=%async_computation.4 | async-start | bytes 8388608
  30.3 69.5 %copy-start.10 = (f32[8,1024]{1,0:T(8,128)}, f32[8,1024]{1,0:T(8,128)S(1)}, u32[]{:S(2)}) copy-start(f32[8,1024]{1,0:T(8,128)S(1)} %broadcast_multiply_fusion.1) | copy-start | bytes 98308
  30.3 19.9 %slice-start.3 = ((s8[4915200]{0:T(1024)(128)(4,1)}), s8[720896]{0:T(1024)(128)(4,1)S(1)}, s32[]{:S(2)}) async-start(s8[4915200]{0:T(1024)(128)(4,1)} %bitcast.226), calls=%async_computation.5 | async-start | bytes 1441792
  48.8 51.1 %copy-start.12 = (f32[8,1024]{1,0:T(8,128)}, f32[8,1024]{1,0:T(8,128)S(1)}, u32[]{:S(2)}) copy-start(f32[8,1024]{1,0:T(8,128)S(1)} %add_rsqrt_fusion.1) | copy-start | bytes 98308
  49.5 73.6 %copy-start.2 = (f32[1024,40]{0,1:T(8,128)}, f32[1024,40]{0,1:T(8,128)S(1)}, u32[]{:S(2)}) copy-start(f32[1024,40]{0,1:T(8,128)S(1)} %get-tuple-element.25) | copy-start | bytes 491524
  49.5 73.6 %copy-start.5 = (f32[1024,40]{0,1:T(8,128)}, f32[1024,40]{0,1:T(8,128)S(1)}, u32[]{:S(2)}) copy-start(f32[1024,40]{0,1:T(8,128)S(1)} %get-tuple-element.26) | copy-start | bytes 491524
  50.2 49.6 %copy-start.18 = (f32[2560]{0:T(1024)}, f32[2560]{0:T(1024)S(1)}, u32[]{:S(2)}) copy-start(f32[2560]{0:T(1024)S(1)} %get-tuple-element.12) | copy-start | bytes 30724
  50.2 49.6 %copy-start.20 = (f32[2560]{0:T(1024)}, f32[2560]{0:T(1024)S(1)}, u32[]{:S(2)}) copy-start(f32[2560]{0:T(1024)S(1)} %get-tuple-element.33) | copy-start | bytes 30724
  99.9 26.6 %copy-start = (pred[1024,1024]{0,1:T(8,128)(4,1)S(1)}, pred[1024,1024]{0,1:T(8,128)(4,1)}, u32[]{:S(2)}) copy-start(pred[1024,1024]{0,1:T(8,128)(4,1)} %iota_compare_fusion) | copy-start | bytes 3145732
  216.5 50.7 %copy-start.11 = (f32[8,1024]{1,0:T(8,128)S(1)}, f32[8,1024]{1,0:T(8,128)}, u32[]{:S(2)}) copy-start(f32[8,1024]{1,0:T(8,128)} %copy-done.10) | copy-start | bytes 98308
  216.5 50.7 %copy-start.13 = (f32[8,1024]{1,0:T(8,128)S(1)}, f32[8,1024]{1,0:T(8,128)}, u32[]{:S(2)}) copy-start(f32[8,1024]{1,0:T(8,128)} %copy-done.12) | copy-start | bytes 98308
  216.5 50.7 %copy-start.19 = (f32[2560]{0:T(1024)S(1)}, f32[2560]{0:T(1024)}, u32[]{:S(2)}) copy-start(f32[2560]{0:T(1024)} %copy-done.18) | copy-start | bytes 30724
  216.5 50.7 %copy-start.21 = (f32[2560]{0:T(1024)S(1)}, f32[2560]{0:T(1024)}, u32[]{:S(2)}) copy-start(f32[2560]{0:T(1024)} %copy-done.20) | copy-start | bytes 30724
  267.2 77.9 %copy-start.9 = (bf16[1,320,2560]{2,1,0:T(8,128)(2,1)S(1)}, bf16[1,320,2560]{2,1,0:T(8,128)(2,1)}, u32[]{:S(2)}) copy-start(bf16[1,320,2560]{2,1,0:T(8,128)(2,1)} %get-tuple-element.24) | copy-start | bytes 4915204
  532.4 1363.5 %all-reduce.5.cloned.1.call-start = ((), (), s32[]{:S(2)}) async-start(), calls=%async_computation.1 | async-start | bytes 83886080 | tf_op jit(solution)/shard_map/psum | solution.py:64
  987.5 18.6 slice-start
  987.5 18.6 copy-start.16
  987.5 18.6 copy-start.17
  987.5 18.5 slice-start.1
  1006.1 49.8 %copy-start.3 = (f32[1024,40]{0,1:T(8,128)S(1)}, f32[1024,40]{0,1:T(8,128)}, u32[]{:S(2)}) copy-start(f32[1024,40]{0,1:T(8,128)} %copy-done.2) | copy-start | bytes 491524
  1006.1 49.8 %copy-start.6 = (f32[1024,40]{0,1:T(8,128)S(1)}, f32[1024,40]{0,1:T(8,128)}, u32[]{:S(2)}) copy-start(f32[1024,40]{0,1:T(8,128)} %copy-done.5) | copy-start | bytes 491524
  1072.7 77.9 %copy-start.4 = (f32[1024,40]{0,1:T(8,128)S(1)}, f32[1024,40]{0,1:T(8,128)}, u32[]{:S(2)}) copy-start(f32[1024,40]{0,1:T(8,128)} %copy-done.2) | copy-start | bytes 491524
  1072.7 77.9 %copy-start.7 = (f32[1024,40]{0,1:T(8,128)S(1)}, f32[1024,40]{0,1:T(8,128)}, u32[]{:S(2)}) copy-start(f32[1024,40]{0,1:T(8,128)} %copy-done.5) | copy-start | bytes 491524
  1072.7 84.5 %copy-start.1 = (pred[1024,1024]{0,1:T(8,128)(4,1)S(1)}, pred[1024,1024]{0,1:T(8,128)(4,1)}, u32[]{:S(2)}) copy-start(pred[1024,1024]{0,1:T(8,128)(4,1)} %iota_compare_fusion) | copy-start | bytes 3145732
  1247.1 50.8 %copy-start.8 = (bf16[1,320,2560]{2,1,0:T(8,128)(2,1)S(1)}, bf16[1,320,2560]{2,1,0:T(8,128)(2,1)}, u32[]{:S(2)}) copy-start(bf16[1,320,2560]{2,1,0:T(8,128)(2,1)} %get-tuple-element.23) | copy-start | bytes 4915204
Sparse Core Ops, SparseCore 0:
  532.5 413.5 all-reduce.2
  1485.1 410.7 all-reduce.4
where the time goes:
time: 1950 us; the launch traced here: 1940 us
  matrix products  828 us (42%)
  waiting for transfers between devices  825 us (42%)
  other arithmetic  249 us (13%)
  local copies, waits for them, and re-layouts  28.4 us (1%)
    psum x2, waiting for transfers between devices, shard_body(): reduced = lax.psum(local_sum, 'tp')  825 us
    dot_general x2, matrix products, layer_partial(): jnp.einsum('bsf,fe->bse', gelu_out, w_down, preferred_element_type=jnp.fl...  306 us
    dot_general x2, matrix products, layer_partial(): jnp.einsum('bsd,df->bsf', normed, w_up, preferred_element_type=jnp.float32)  156 us
    dot_general x2, matrix products, layer_partial(): jnp.einsum('bgrst,btgd->bgrsd', attn_probs, values, preferred_element_typ...  101 us
    dot_general x2, matrix products, layer_partial(): jnp.einsum('bsd,dgc->bsgc', normed, w_qkv, preferred_element_type=jnp.flo...  99.4 us
    dot_general x2, matrix products, layer_partial(): jnp.einsum('bsgrd,btgd->bgrst', query, keys, preferred_element_type=jnp.f...  97.3 us
    reduce_sum x2, other arithmetic, layer_partial(): attn_probs = jax.nn.softmax(scores, axis=-1).astype(jnp.bfloat16)  82.6 us
    dot_general x2, matrix products, layer_partial(): jnp.einsum('bgrsd,grde->bse', context, out_heads, preferred_element_type=...  68.3 us
  transfers between devices with their start and end apart: 2, of which 2 were waited for; matrix products, arithmetic and copies ran while one was open for 0% of the time, Pallas kernels for 0%

commit v1 on v0

v1 whole, which is shorter than its diff:
```python
import functools

import jax
import jax.numpy as jnp
import numpy as np
from jax import lax
from jax.experimental import pallas as pl
from jax.experimental.pallas import tpu as pltpu
from jax.sharding import PartitionSpec as P

LN_EPS = 1e-5
ROPE_BASE = 10000.0
F32 = jnp.float32
BF16 = jnp.bfloat16
MESH = pl.DeviceIdType.MESH
VMEM_LIMIT = 67043328

CORES = 2
ROWS = 256
LANES = 128
SLOT = 40


def rope_tables(seq_len, head_dim):
    half_dim = head_dim // 2
    inv_freq = (ROPE_BASE ** (-2.0 * np.arange(half_dim, dtype=np.float32) / head_dim)).astype(np.float32)
    angles = np.arange(seq_len, dtype=np.float32)[:, None] * inv_freq[None, :]
    cos_tab = np.ones((seq_len, LANES), np.float32)
    sin_tab = np.zeros((seq_len, LANES), np.float32)
    for k in range(2):
        cos_tab[:, k * half_dim:(k + 1) * half_dim] = np.cos(angles)
        sin_tab[:, k * half_dim:(k + 1) * half_dim] = np.sin(angles)
    return cos_tab, sin_tab


def prep_qkv(w_qkv, head_dim):
    layers, d_model, heads, _ = w_qkv.shape
    half_dim = head_dim // 2
    w = w_qkv.reshape(layers, d_model, heads, 3, 2, half_dim)
    w = jnp.transpose(w, (0, 2, 1, 4, 3, 5)).reshape(layers, heads, d_model, 2, 3 * half_dim)
    w = jnp.pad(w, ((0, 0),) * 4 + ((0, LANES - 3 * half_dim),))
    return w.reshape(layers, heads, d_model, 2 * LANES)


def prep_out(w_out, heads, head_dim):
    layers, _, d_model = w_out.shape
    half_dim = head_dim // 2
    w = w_out.reshape(layers, heads, 2, half_dim, d_model)
    first = jnp.transpose(w[:, :3], (0, 2, 1, 3, 4)).reshape(layers, 2, 3 * half_dim, d_model)
    first = jnp.pad(first, ((0, 0), (0, 0), (0, LANES - 3 * half_dim), (0, 0)))
    second = jnp.pad(w[:, 3], ((0, 0), (0, 0), (half_dim, LANES - 2 * half_dim), (0, 0)))
    return jnp.concatenate([first, second], axis=1).reshape(layers, 4 * LANES, d_model)


def body(cfg, act, w_q, w_o, w_u, w_d, gain, bias, cos_v, sin_v,
         out, st_q, st_o, st_u, st_d,
         x_v, n_v, q_v, kv_v, cu_v, p_v, wq_v, wu_v, wod_v,
         a1r, a2r, br, comb, ysh, xres,
         s_a1s, s_a1r, s_a2s, s_a2r, s_bs, s_br, s_cs, s_cr, s_ds, s_dr, s_yl, s_x, s_xr, s_f, s_wl, s_ws, s_wr):
    n_chip, layers, heads, head_dim, d_model, ff, items, blocks = cfg
    seq_blocks = blocks
    half_dim = head_dim // 2
    total = layers * items
    tp = lax.axis_index("tp")
    chip = lax.div(tp, CORES)
    core = lax.rem(tp, CORES)
    right = {"tp": lax.rem(chip + 1, n_chip) * CORES + core}
    left = {"tp": lax.rem(chip + n_chip - 1, n_chip) * CORES + core}
    mate = {"tp": chip * CORES + (CORES - 1 - core)}
    own_base = core * (items * ROWS)
    shard = ROWS // n_chip
    hs = shard // 2
    ow = 4 * LANES

    def ring(k):
        return lax.rem(chip + k, n_chip)

    def remote(src, dst, ssem, rsem, dev):
        return pltpu.make_async_remote_copy(src_ref=src, dst_ref=dst, send_sem=ssem, recv_sem=rsem, device_id=dev, device_id_type=MESH)

    def sh_rows(k, off, size):
        return pl.ds(pl.multiple_of(ring(k) * shard + off, hs), size)

    def y_rows(t, k, off, size):
        base = own_base + lax.rem(t, items) * ROWS
        return pl.ds(pl.multiple_of(base + ring(k) * shard + off, hs), size)

    def item_rows(t):
        return pl.ds(pl.multiple_of(own_base + lax.rem(t, items) * ROWS, ROWS), ROWS)

    def w_dst(h):
        return [wq_v.at[pl.ds(h * heads, heads)], wu_v.at[h], wod_v.at[pl.ds(h * ow, ow)], wod_v.at[pl.ds(2 * ow + h * ff, ff)]]

    def w_src(l):
        return [w_q.at[l], w_u.at[l], w_o.at[l], w_d.at[l]]

    staged = [st_q, st_u, st_o, st_d]

    def own_load(l):
        return [pltpu.make_async_copy(s, d, s_wl.at[0, i]) for i, (s, d) in enumerate(zip(w_src(l), w_dst(0)))]

    def mate_load():
        return [pltpu.make_async_copy(s, d, s_wl.at[1, i]) for i, (s, d) in enumerate(zip(staged, w_dst(1)))]

    def push_first():
        return [remote(s, d, s_ws.at[0, i], s_wr.at[0, i], mate) for i, (s, d) in enumerate(zip(w_src(0), w_dst(1)))]

    def push_second():
        return [remote(s, d, s_ws.at[1, i], s_wr.at[1, i], mate) for i, (s, d) in enumerate(zip(w_src(1), staged))]

    def wait_weights(t, idx):
        @pl.when(t == 0)
        def _():
            for i in idx:
                own_load(0)[i].wait()
                push_first()[i].wait_recv()

        @pl.when(t == items)
        def _():
            for i in idx:
                own_load(1)[i].wait()
                mate_load()[i].wait()

    def x_load(t):
        @pl.when(t < items)
        def _():
            pltpu.make_async_copy(act.at[item_rows(t)], x_v, s_x).start()

        @pl.when(t >= items)
        def _():
            pltpu.make_async_copy(out.at[item_rows(t)], x_v, s_x).start()

    def x_wait():
        pltpu.make_async_copy(act.at[pl.ds(0, ROWS)], x_v, s_x).wait()

    def xres_load(t):
        sl = lax.rem(t, 2)

        @pl.when(t < items)
        def _():
            pltpu.make_async_copy(act.at[y_rows(t, 0, 0, shard)], xres.at[sl], s_xr.at[sl]).start()

        @pl.when(t >= items)
        def _():
            pltpu.make_async_copy(out.at[y_rows(t, 0, 0, shard)], xres.at[sl], s_xr.at[sl]).start()

    def xres_wait(t):
        sl = lax.rem(t, 2)
        pltpu.make_async_copy(act.at[pl.ds(0, shard)], xres.at[sl], s_xr.at[sl]).wait()

    def a_copies(t):
        sl, s3 = lax.rem(t, 2), lax.rem(t, 3)
        return [
            remote(p_v.at[sl, sh_rows(2, 0, hs)], a1r.at[sl, 0], s_a1s.at[sl, 0], s_a1r.at[sl, 0], right),
            remote(p_v.at[sl, sh_rows(2, hs, hs)], a1r.at[sl, 1], s_a1s.at[sl, 1], s_a1r.at[sl, 1], left),
            remote(p_v.at[sl, sh_rows(1, hs, hs)], a2r.at[s3, 0], s_a2s.at[sl, 0], s_a2r.at[s3, 0], right),
            remote(p_v.at[sl, sh_rows(n_chip - 1, 0, hs)], a2r.at[s3, 1], s_a2s.at[sl, 1], s_a2r.at[s3, 1], left),
        ]

    def b_copies(t):
        sl = lax.rem(t, 2)
        return [
            remote(comb.at[sl, 0], br.at[sl, 0], s_bs.at[sl, 0], s_br.at[sl, 0], right),
            remote(comb.at[sl, 1], br.at[sl, 1], s_bs.at[sl, 1], s_br.at[sl, 1], left),
        ]

    def c_copies(t):
        sl = lax.rem(t, 2)
        rows = y_rows(t, 0, 0, shard)
        return [
            remote(ysh.at[sl], out.at[rows], s_cs.at[sl, 0], s_cr.at[sl, 0], right),
            remote(ysh.at[sl], out.at[rows], s_cs.at[sl, 1], s_cr.at[sl, 1], left),
        ]

    def y_local(t):
        sl = lax.rem(t, 2)
        return pltpu.make_async_copy(ysh.at[sl], out.at[y_rows(t, 0, 0, shard)], s_yl.at[sl])

    def d_copies(t):
        sl = lax.rem(t, 2)
        from_left = y_rows(t, n_chip - 1, 0, hs)
        from_right = y_rows(t, 1, hs, hs)
        return [
            remote(out.at[from_left], out.at[from_left], s_ds.at[sl, 0], s_dr.at[sl, 0], right),
            remote(out.at[from_right], out.at[from_right], s_ds.at[sl, 1], s_dr.at[sl, 1], left),
        ]

    def f_copy(t):
        rows = item_rows(t)
        return remote(out.at[rows], out.at[rows], s_f.at[0], s_f.at[1], mate)

    def phase_a(t):
        for c in a_copies(t):
            c.start()
        xres_load(t)

    def phase_b(t):
        sl = lax.rem(t, 2)

        @pl.when(t >= 2)
        def _():
            for c in b_copies(t - 2):
                c.wait_send()
        first = a_copies(t)
        first[0].wait_recv()
        first[1].wait_recv()
        comb[sl, 0] = (p_v[sl, sh_rows(1, 0, hs), :].astype(F32) + a1r[sl, 0].astype(F32)).astype(BF16)
        comb[sl, 1] = (p_v[sl, sh_rows(n_chip - 1, hs, hs), :].astype(F32) + a1r[sl, 1].astype(F32)).astype(BF16)
        for c in b_copies(t):
            c.start()

    def phase_c(t):
        sl, s3 = lax.rem(t, 2), lax.rem(t, 3)
        a = a_copies(t)
        b = b_copies(t)
        for c in a:
            c.wait_send()
        a[2].wait_recv()
        a[3].wait_recv()
        b[0].wait_recv()
        b[1].wait_recv()
        xres_wait(t)
        for k in range(2):
            rows = pl.ds(k * hs, hs)
            summed = p_v[sl, sh_rows(0, k * hs, hs), :].astype(F32) + br[sl, k].astype(F32) + a2r[s3, 1 - k].astype(F32)
            ysh[sl, rows, :] = (xres[sl, rows, :].astype(F32) + summed.astype(BF16).astype(F32)).astype(BF16)
        for c in c_copies(t):
            c.start()
        y_local(t).start()

    def phase_d(t):
        for c in c_copies(t):
            c.wait_recv()
        y_local(t).wait()
        for c in d_copies(t):
            c.start()

    def phase_e(t):
        for c in d_copies(t):
            c.wait_recv()
            c.wait_send()
        for c in c_copies(t):
            c.wait_send()

        @pl.when(t >= items)
        def _():
            f_copy(t).start()

    lane = lax.broadcasted_iota(jnp.int32, (ROWS, LANES), 1)

    def layer_norm(l):
        step = 64

        @pl.loop(0, ROWS // step)
        def _(i):
            r = pl.ds(pl.multiple_of(i * step, step), step)
            xf = x_v[r, :].astype(F32)
            mean = jnp.mean(xf, axis=-1, keepdims=True)
            centered = xf - mean
            var = jnp.mean(centered * centered, axis=-1, keepdims=True)
            n_v[r, :] = (centered * lax.rsqrt(var + LN_EPS) * gain[pl.ds(l, 1), :] + bias[pl.ds(l, 1), :]).astype(BF16)

    def qkv(blk):
        rows = pl.ds(pl.multiple_of(blk * ROWS, ROWS), ROWS)
        for g in range(2 * heads):
            y = jnp.dot(n_v[...], wq_v[g], preferred_element_type=F32)
            t0, t1 = y[:, :LANES], y[:, LANES:]
            cs, sn = cos_v[rows, :], sin_v[rows, :]
            for k, v in enumerate((t0 * cs - t1 * sn, t1 * cs + t0 * sn)):
                cols = pl.ds(k * LANES, LANES)
                q_v[g, :, cols] = jnp.where(lane < half_dim, v, 0.0).astype(BF16)
                kv_v[g, rows, cols] = pltpu.roll(v, LANES - half_dim, 1).astype(BF16)

    def attend(g, n):
        scores = lax.dot_general(q_v[g], kv_v[g, :n, :], (((1,), (1,)), ((), ())), preferred_element_type=F32)
        scores = scores * (head_dim ** -0.5 * np.log2(np.e))
        ri = lax.broadcasted_iota(jnp.int32, (ROWS, ROWS), 0)
        ci = lax.broadcasted_iota(jnp.int32, (ROWS, ROWS), 1)
        diag = jnp.where(ri >= ci, scores[:, n - ROWS:], -1e30)
        scores = jnp.concatenate([scores[:, :n - ROWS], diag], axis=1) if n > ROWS else diag
        e = jnp.exp2(scores - jnp.max(scores, axis=1, keepdims=True))
        probs = (e * (1.0 / jnp.sum(e, axis=1, keepdims=True))).astype(BF16)
        return jnp.dot(probs, kv_v[g, :n, :], preferred_element_type=F32)

    def attention(blk):
        for i in range(seq_blocks):
            @pl.when(blk == i)
            def _():
                n = (i + 1) * ROWS

                @pl.loop(0, 2)
                def _(h):
                    base = pl.multiple_of(h * ow, ow)
                    acc = [None, None]
                    for j in range(heads):
                        ctx = attend(h * heads + j, n)
                        for k in range(2):
                            c = ctx[:, k * LANES:(k + 1) * LANES]
                            if j == 0:
                                acc[k] = pltpu.roll(c, LANES - half_dim, 1)
                            elif j == 1:
                                acc[k] = jnp.where(lane < half_dim, acc[k], c)
                            elif j == 2:
                                c = pltpu.roll(c, half_dim, 1)
                                v = jnp.where(lane < 2 * half_dim, acc[k], jnp.where(lane < 3 * half_dim, c, 0.0))
                                cu_v[:, pl.ds(base + k * LANES, LANES)] = v.astype(BF16)
                            else:
                                v = jnp.where((lane >= half_dim) & (lane < 2 * half_dim), c, 0.0)
                                cu_v[:, pl.ds(base + (2 + k) * LANES, LANES)] = v.astype(BF16)

    def up():
        tile = 256
        for h in range(2):
            for n in range(ff // tile):
                y = jnp.dot(n_v[...], wu_v[h, :, n * tile:(n + 1) * tile], preferred_element_type=F32)
                u = 0.5 * y * (1.0 + lax.erf(y * np.float32(0.5 ** 0.5)))
                c = 2 * ow + h * ff + n * tile
                cu_v[:, c:c + tile] = u.astype(BF16)

    def down(t):
        tile = 256
        sl = lax.rem(t, 2)
        for n in range(d_model // tile):
            y = jnp.dot(cu_v[...], wod_v[:, n * tile:(n + 1) * tile], preferred_element_type=F32)
            p_v[sl, :, n * tile:(n + 1) * tile] = y.astype(BF16)

    barrier = pltpu.get_barrier_semaphore()
    for dev in (left, right, mate):
        pl.semaphore_signal(barrier, inc=1, device_id=dev, device_id_type=MESH)
    x_load(jnp.int32(0))
    for c in own_load(0):
        c.start()
    pl.semaphore_wait(barrier, 3)
    for c in push_first():
        c.start()

    @pl.loop(0, total + 4)
    def _(t):
        compute = t < total

        @pl.when(t == items)
        def _():
            for c in push_second():
                c.wait_recv()
            for c in own_load(1) + mate_load():
                c.start()

        @pl.when(compute)
        def _():
            x_wait()
            layer_norm(lax.div(t, items))

            @pl.when(t + 1 < total)
            def _():
                x_load(t + 1)

            blk = lax.rem(t, seq_blocks)
            wait_weights(t, [0])
            qkv(blk)
            attention(blk)
            wait_weights(t, [1])
            up()

        @pl.when(t == 2)
        def _():
            for c in push_second():
                c.start()

        @pl.when(t >= 4)
        def _():
            phase_e(t - 4)

        @pl.when((t >= 3) & (t < total + 3))
        def _():
            phase_d(t - 3)

        @pl.when((t >= 2) & (t < total + 2))
        def _():
            phase_c(t - 2)

        @pl.when(compute)
        def _():
            wait_weights(t, [2, 3])
            down(t)
            phase_a(t)

        @pl.when((t >= 1) & (t < total + 1))
        def _():
            phase_b(t - 1)

    for t in (total - 2, total - 1):
        for c in b_copies(jnp.int32(t)):
            c.wait_send()
    for c in push_first() + push_second():
        c.wait_send()
    half_rows = items * ROWS
    mine = out.at[pl.ds(pl.multiple_of(own_base, ROWS), half_rows)]
    every = remote(mine, mine, s_f.at[0], s_f.at[1], mate)
    every.wait_send()
    every.wait_recv()


def solution(mesh):
    n_tp = mesh.shape["tp"]
    n_chip = n_tp // CORES

    def shard_body(act_in, ln_gain, ln_bias, w_qkv, w_out, w_up, w_down):
        batch, seq_len, d_model = act_in.shape
        layers, _, heads, group_cols = w_qkv.shape
        head_dim = w_out.shape[1] // heads
        ff = w_up.shape[2]
        assert group_cols == 3 * head_dim and heads == 4 and head_dim == 2 * SLOT
        items = batch * seq_len // (CORES * ROWS)
        blocks = seq_len // ROWS
        cfg = (n_chip, layers, heads, head_dim, d_model, ff, items, blocks)
        shard = ROWS // n_chip
        ow = 4 * LANES
        w_q = prep_qkv(w_qkv, head_dim)
        w_o = prep_out(w_out, heads, head_dim)
        cos_tab, sin_tab = rope_tables(seq_len, head_dim)
        vm = pl.BlockSpec(memory_space=pltpu.VMEM)
        hb = pl.BlockSpec(memory_space=pl.ANY)
        dma = pltpu.SemaphoreType.DMA
        res = pl.pallas_call(
            functools.partial(body, cfg),
            name="layers",
            out_shape=[
                jax.ShapeDtypeStruct((batch * seq_len, d_model), BF16),
                jax.ShapeDtypeStruct((heads, d_model, 2 * LANES), BF16),
                jax.ShapeDtypeStruct((ow, d_model), BF16),
                jax.ShapeDtypeStruct((d_model, ff), BF16),
                jax.ShapeDtypeStruct((ff, d_model), BF16),
            ],
            in_specs=[hb] * 5 + [vm] * 4,
            out_specs=[hb] * 5,
            scratch_shapes=[
                pltpu.VMEM((ROWS, d_model), BF16),
                pltpu.VMEM((ROWS, d_model), BF16),
                pltpu.VMEM((2 * heads, ROWS, 2 * LANES), BF16),
                pltpu.VMEM((2 * heads, seq_len, 2 * LANES), BF16),
                pltpu.VMEM((ROWS, 2 * ow + 2 * ff), BF16),
                pltpu.VMEM((2, ROWS, d_model), BF16),
                pltpu.VMEM((2 * heads, d_model, 2 * LANES), BF16),
                pltpu.VMEM((2, d_model, ff), BF16),
                pltpu.VMEM((2 * ow + 2 * ff, d_model), BF16),
                pltpu.VMEM((2, 2, shard // 2, d_model), BF16),
                pltpu.VMEM((3, 2, shard // 2, d_model), BF16),
                pltpu.VMEM((2, 2, shard // 2, d_model), BF16),
                pltpu.VMEM((2, 2, shard // 2, d_model), BF16),
                pltpu.VMEM((2, shard, d_model), BF16),
                pltpu.VMEM((2, shard, d_model), BF16),
                dma((2, 2)), dma((2, 2)), dma((2, 2)), dma((3, 2)), dma((2, 2)), dma((2, 2)),
                dma((2, 2)), dma((2, 2)), dma((2, 2)), dma((2, 2)),
                dma((2,)), dma, dma((2,)), dma((2,)), dma((2, 4)), dma((2, 4)), dma((2, 4)),
            ],
            compiler_params=pltpu.CompilerParams(collective_id=0, has_side_effects=True, vmem_limit_bytes=VMEM_LIMIT),
        )(act_in.reshape(batch * seq_len, d_model), w_q, w_o, w_up, w_down, ln_gain, ln_bias, jnp.asarray(cos_tab), jnp.asarray(sin_tab))
        return res[0].reshape(batch, seq_len, d_model)

    return jax.shard_map(shard_body, mesh=mesh, in_specs=(P("dp", None, None), P(None, None), P(None, None), P(None, None, "tp", None), P(None, "tp", None), P(None, None, "tp"), P(None, "tp", None)), out_specs=P("dp", None, None), check_vma=False)
```

time: 1950 us -> 805 us (0.41)
  matrix products: 828 us -> 0 us
  waiting for transfers between devices: 825 us -> 0 us
  Pallas kernels: 0 us -> 738 us
  other arithmetic: 249 us -> 3 us
  local copies, waits for them, and re-layouts: 28.4 us -> 63.3 us
    dot_general x12 -> x0, matrix products: 828 us -> none  [the longest x2 306 us: layer_partial(): jnp.einsum('bsf,fe->bse', gelu_out, w_down, preferred_element_type=jnp.fl...]
    psum x2 -> x0, waiting for transfers between devices: 825 us -> none  [shard_body(): reduced = lax.psum(local_sum, 'tp')]
    pallas_call x0 -> x1, Pallas kernels: none -> 738 us  [shard_body(): pl.pallas_call(functools.partial(body, cfg), name='layers', out_shape=[ja...]
    reduce_sum x6 -> x0, other arithmetic: 175 us -> none  [the longest x2 82.6 us: layer_partial(): attn_probs = jax.nn.softmax(scores, axis=-1).astype(jnp.bfloat16)]
    convert_element_type x1 -> x0, other arithmetic: 41.3 us -> none  [shard_body(): (hidden.astype(jnp.float32) + reduced.astype(jnp.float32)).astype(jnp.bfl...]
    unnamed x52 -> x1, local copies, waits for them, and re-layouts: 0.11 us -> 29 us
  transfers between devices with their start and end apart: 2 -> 0, of which waited for: 2 -> 0; matrix products, arithmetic and copies ran while one was open for 0% -> 0% of each run, Pallas kernels for 0% -> 0%
where the time goes in v1:
time: 805 us
  Pallas kernels  738 us (92%)
  local copies, waits for them, and re-layouts  63.3 us (8%)
    pallas_call x1, Pallas kernels, shard_body(): pl.pallas_call(functools.partial(body, cfg), name='layers', out_shape=[ja...  738 us
    unnamed x1, local copies, waits for them, and re-layouts  29 us

profile of v1, /device:TPU:113, one launch (start us, length us, event | category | flops | bytes accessed | tf_op | source)
XLA Modules:
  0.0 804.6 jit_solution(17993159198283046894)
XLA Ops:
  0.0 1.2 slice_bitcast_fusion.1
  1.2 1.9 slice_bitcast_fusion
  3.1 0.2 copy.18
  3.3 3.0 fusion.2
  6.3 8.4 %copy.16 = bf16[2,4,2560,2,3,40]{2,5,4,3,1,0:T(8,128)(2,1)} copy(bf16[2,4,2560,2,3,40]{2,5,3,4,1,0:T(8,128)(2,1)} %bitcast.21) | data formatting | bytes 19660800 | tf_op jit(solution)/shard_map/transpose | solution.py:40
  14.7 9.0 %pad.12 = bf16[2,4,2560,2,128]{2,4,3,1,0:T(8,128)(2,1)} pad(bf16[2,4,2560,2,120]{2,4,3,1,0:T(8,128)(2,1)} %bitcast.19, bf16[]{:T(256)} %constant.6.clone.1), padding=0_0x0_0x0_0x0_0x0_8 | pad | bytes 20316162 | tf_op jit(solution)/shard_map/jit(_pad)/pad | solution.py:41
  23.6 13.8 %copy.20.w_q = bf16[2,4,2560,256]{3,2,1,0:T(8,128)(2,1)} copy(bf16[2,4,2560,256]{2,3,1,0:T(8,128)(2,1)} %bitcast.18) | data formatting | bytes 20971520 | tf_op jit(solution)/shard_map/reshape | solution.py:42
  37.4 738.2 %layers.1 = (bf16[8192,2560]{1,0:T(8,128)(2,1)}, bf16[4,2560,256]{2,1,0:T(8,128)(2,1)}, bf16[512,2560]{1,0:T(8,128)(2,1)}, bf16[2560,1280]{1,0:T(8,128)(2,1)}, bf16[1280,2560]{1,0:T(8,128)(2,1)}) custom-call(bf16[8192,2560]{1,0:T(8,128)(2,1)} %bitcast.16, bf16[2,4,2560,256]{3,2,1,0:T(8,128)(2,1)} %copy.20.w_q, bf16[2,512,2560]{2,1,0:T(8,128)(2,1)} %bitcast.20, ...), custom_call_target="tpu_custom_call" | custom-call | tf_op jit(solution)/shard_map/layers/pallas_call | solution.py:424
  775.6 29.0 %copy.23 = bf16[8,1024,2560]{2,1,0:T(8,128)(2,1)} copy(bf16[8,1024,2560]{2,1,0:T(8,128)(2,1)} %bitcast.17) | data formatting | bytes 83886080

commit v2 on v1

v2 whole, which is shorter than its diff:
```python
import functools

import jax
import jax.numpy as jnp
import numpy as np
from jax import lax
from jax.experimental import pallas as pl
from jax.experimental.pallas import tpu as pltpu
from jax.sharding import PartitionSpec as P

LN_EPS = 1e-5
ROPE_BASE = 10000.0
F32 = jnp.float32
BF16 = jnp.bfloat16
MESH = pl.DeviceIdType.MESH
VMEM_LIMIT = 67043328

CORES = 2
ROWS = 256
LANES = 128
SLOT = 40


def rope_tables(seq_len, head_dim):
    half_dim = head_dim // 2
    inv_freq = (ROPE_BASE ** (-2.0 * np.arange(half_dim, dtype=np.float32) / head_dim)).astype(np.float32)
    angles = np.arange(seq_len, dtype=np.float32)[:, None] * inv_freq[None, :]
    cos_tab = np.ones((seq_len, LANES), np.float32)
    sin_tab = np.zeros((seq_len, LANES), np.float32)
    for k in range(2):
        cos_tab[:, k * half_dim:(k + 1) * half_dim] = np.cos(angles)
        sin_tab[:, k * half_dim:(k + 1) * half_dim] = np.sin(angles)
    return cos_tab, sin_tab


def regroup(head_dim):
    half_dim = head_dim // 2
    sel = np.zeros((3 * head_dim, 2 * LANES), np.float32)
    for part in range(3):
        for half in range(2):
            for i in range(half_dim):
                sel[(part * 2 + half) * half_dim + i, half * LANES + part * half_dim + i] = 1.0
    return sel


def body(cfg, act, w_q, w_o, w_u, w_d, gain, bias, cos_v, sin_v, sel_v,
         out, wu_v, wod_v, st_q, st_o, st_u, st_d, pq, po,
         stg, pst, pm, x_v, n_v, q_v, kv_v, cu_v, p_v, wq_v,
         a1r, a2r, br, comb, ysh, xres,
         s_a1s, s_a1r, s_a2s, s_a2r, s_bs, s_br, s_cs, s_cr, s_ds, s_dr, s_yl, s_x, s_xr, s_f, s_wl, s_ws, s_wr, s_stg, s_pm, s_pq, s_rl, s_fin):
    n_chip, layers, heads, head_dim, d_model, ff, items, blocks, late = cfg
    side_at = 3
    seq_blocks = blocks
    group_cols = 3 * head_dim
    half_dim = head_dim // 2
    total = layers * items
    tp = lax.axis_index("tp")
    chip = lax.div(tp, CORES)
    core = lax.rem(tp, CORES)
    right = {"tp": lax.rem(chip + 1, n_chip) * CORES + core}
    left = {"tp": lax.rem(chip + n_chip - 1, n_chip) * CORES + core}
    mate = {"tp": chip * CORES + (CORES - 1 - core)}
    own_base = core * (items * ROWS)
    mate_base = (CORES - 1 - core) * (items * ROWS)
    shard = ROWS // n_chip
    hs = shard // 2
    ow = 4 * LANES
    hw = ow + ff

    def ring(k):
        return lax.rem(chip + k, n_chip)

    def remote(src, dst, ssem, rsem, dev):
        return pltpu.make_async_remote_copy(src_ref=src, dst_ref=dst, send_sem=ssem, recv_sem=rsem, device_id=dev, device_id_type=MESH)

    def sh_rows(k, off, size):
        return pl.ds(pl.multiple_of(ring(k) * shard + off, hs), size)

    def y_rows(t, k, off, size):
        base = own_base + lax.rem(t, items) * ROWS
        return pl.ds(pl.multiple_of(base + ring(k) * shard + off, hs), size)

    def item_rows(t):
        return pl.ds(pl.multiple_of(own_base + lax.rem(t, items) * ROWS, ROWS), ROWS)

    def ud_dst(h):
        return [wu_v.at[:, pl.ds(h * ff, ff)], wod_v.at[pl.ds(h * hw + ow, ff)]]

    def own_ud(l):
        return [pltpu.make_async_copy(s.at[l], d, s_wl.at[0, i]) for i, (s, d) in enumerate(zip((w_u, w_d), ud_dst(0)))]

    def mate_ud():
        return [pltpu.make_async_copy(s, d, s_wl.at[1, i]) for i, (s, d) in enumerate(zip((st_u, st_d), ud_dst(1)))]

    def push(l, i):
        src = (w_q, w_o, w_u, w_d)[i].at[l]
        dst = (st_q.at[l], st_o.at[l], st_u if l else ud_dst(1)[0], st_d if l else ud_dst(1)[1])[i]
        return remote(src, dst, s_ws.at[l, i], s_wr.at[l, i], mate)

    def regroup_q(src, dst):
        for c in range(0, d_model, 512):
            y = lax.dot_general(src[:, c:c + 512], sel_v[...], (((0,), (0,)), ((), ())), preferred_element_type=F32)
            dst[c:c + 512, :] = y.astype(BF16)

    def regroup_o(src, dst):
        for c in range(0, d_model, 512):
            y = lax.dot_general(sel_v[...], src[:, c:c + 512], (((0,), (0,)), ((), ())), preferred_element_type=F32)
            dst[:, c:c + 512] = y.astype(BF16)

    slots = (stg.at[0], stg.at[1], cu_v.at[pl.ds(0, group_cols), pl.ds(0, d_model)])

    def q_copy(h, g):
        k = g % len(slots)
        return pltpu.make_async_copy((w_q, st_q)[h].at[0, g], slots[k], s_stg.at[k])

    def load_q(h):
        for g in range(heads):
            q_copy(0, g).wait()
            regroup_q(slots[g % len(slots)], wq_v.at[h * heads + g])
            if g + len(slots) < heads:
                @pl.when(h == 0)
                def _():
                    q_copy(0, g + len(slots)).start()

                @pl.when(h == 1)
                def _():
                    q_copy(1, g + len(slots)).start()

    def o_copy(l, h, k):
        rows = (pl.ds(0, group_cols), pl.ds(group_cols, head_dim))[k]
        return pltpu.make_async_copy((w_o, st_o)[h].at[l, rows], stg.at[k, pl.ds(0, (group_cols, head_dim)[k])], s_stg.at[k])

    def clear_tail():
        stg[1, head_dim:, :] = jnp.zeros((group_cols - head_dim, d_model), BF16)

    def start_o(h):
        clear_tail()

        @pl.when(h == 0)
        def _():
            for k in range(2):
                o_copy(0, 0, k).start()

        @pl.when(h == 1)
        def _():
            for k in range(2):
                o_copy(0, 1, k).start()

    def load_o(h):
        for k in range(2):
            o_copy(0, 0, k).wait()

        @pl.loop(0, 2)
        def _(k):
            regroup_o(stg.at[k], wod_v.at[pl.ds(pl.multiple_of(h * hw + k * 2 * LANES, 2 * LANES), 2 * LANES)])

    n_side = 2 * heads + 4

    def side_copy(a):
        for h in range(2):
            @pl.when((a >= h * heads) & (a < (h + 1) * heads))
            def _():
                sl = lax.rem(a, 2)
                pltpu.make_async_copy((w_q, st_q)[h].at[1, a - h * heads], stg.at[sl], s_stg.at[sl]).start()

            for k in range(2):
                @pl.when(a == 2 * heads + 2 * h + k)
                def _():
                    o_copy(1, h, k).start()

    def pq_copy(g):
        return pltpu.make_async_copy(pst, pq.at[g], s_pq.at[0])

    def po_copy(b):
        return pltpu.make_async_copy(pm, po.at[pl.ds(pl.multiple_of(b * 2 * LANES, 2 * LANES), 2 * LANES)], s_pq.at[1])

    def side_job(a):
        sl = lax.rem(a, 2)

        @pl.when(a == heads - 1)
        def _():
            push(1, 0).wait_recv()

        @pl.when(a == 2 * heads + 1)
        def _():
            push(1, 1).wait_recv()

        @pl.when(a < 2 * heads)
        def _():
            pltpu.make_async_copy(w_q.at[1, 0], stg.at[sl], s_stg.at[sl]).wait()

            @pl.when(a > 0)
            def _():
                pq_copy(a - 1).wait()

            regroup_q(stg.at[sl], pst)
            pq_copy(a).start()

        @pl.when(a >= 2 * heads)
        def _():
            for k in range(2):
                @pl.when(sl == k)
                def _():
                    o_copy(1, 0, k).wait()

            @pl.when(a > 2 * heads)
            def _():
                po_copy(a - 2 * heads - 1).wait()

            regroup_o(stg.at[sl], pm)
            po_copy(a - 2 * heads).start()

        @pl.when(a == 2 * heads)
        def _():
            clear_tail()

        @pl.when(a + 1 < n_side)
        def _():
            side_copy(a + 1)

    def load_second(k):
        if k == 0:
            return [pltpu.make_async_copy(pq, wq_v, s_rl.at[0])]
        if k == 1:
            return [own_ud(1)[0], mate_ud()[0]]
        outs = [pltpu.make_async_copy(po.at[pl.ds(h * ow, ow)], wod_v.at[pl.ds(h * hw, ow)], s_rl.at[1 + h]) for h in range(2)]
        return [own_ud(1)[1], mate_ud()[1]] + outs

    def wait_ud(i, k):
        @pl.when(i == 0)
        def _():
            own_ud(0)[k].wait()

        @pl.when(i == 2)
        def _():
            push(0, 2 + k).wait_recv()

        @pl.when(i == items + 1)
        def _():
            for c in load_second(1 + k):
                c.wait()

    def x_load(i):
        t = i - 1

        @pl.when(i == 0)
        def _():
            pltpu.make_async_copy(act.at[pl.ds(pl.multiple_of(mate_base, ROWS), ROWS)], x_v, s_x).start()

        @pl.when((i >= 1) & (t < items))
        def _():
            pltpu.make_async_copy(act.at[item_rows(t)], x_v, s_x).start()

        @pl.when(t >= items)
        def _():
            pltpu.make_async_copy(out.at[item_rows(t)], x_v, s_x).start()

    def x_wait():
        pltpu.make_async_copy(act.at[pl.ds(0, ROWS)], x_v, s_x).wait()

    def xres_load(t):
        sl = lax.rem(t, 2)

        @pl.when(t < items)
        def _():
            pltpu.make_async_copy(act.at[y_rows(t, 0, 0, shard)], xres.at[sl], s_xr.at[sl]).start()

        @pl.when(t >= items)
        def _():
            pltpu.make_async_copy(out.at[y_rows(t, 0, 0, shard)], xres.at[sl], s_xr.at[sl]).start()

    def xres_wait(t):
        sl = lax.rem(t, 2)
        pltpu.make_async_copy(act.at[pl.ds(0, shard)], xres.at[sl], s_xr.at[sl]).wait()

    def a_copies(t):
        sl = lax.rem(t, 2)
        return [
            remote(p_v.at[sh_rows(2, 0, hs)], a1r.at[sl, 0], s_a1s.at[sl, 0], s_a1r.at[sl, 0], right),
            remote(p_v.at[sh_rows(2, hs, hs)], a1r.at[sl, 1], s_a1s.at[sl, 1], s_a1r.at[sl, 1], left),
            remote(p_v.at[sh_rows(1, hs, hs)], a2r.at[sl, 0], s_a2s.at[sl, 0], s_a2r.at[sl, 0], right),
            remote(p_v.at[sh_rows(n_chip - 1, 0, hs)], a2r.at[sl, 1], s_a2s.at[sl, 1], s_a2r.at[sl, 1], left),
        ]

    def b_copies(t):
        sl = lax.rem(t, 2)
        return [
            remote(comb.at[sl, 0], br.at[sl, 0], s_bs.at[sl, 0], s_br.at[sl, 0], right),
            remote(comb.at[sl, 1], br.at[sl, 1], s_bs.at[sl, 1], s_br.at[sl, 1], left),
        ]

    def c_copies(t):
        sl = lax.rem(t, 2)
        rows = y_rows(t, 0, 0, shard)
        return [
            remote(ysh.at[sl], out.at[rows], s_cs.at[sl, 0], s_cr.at[sl, 0], right),
            remote(ysh.at[sl], out.at[rows], s_cs.at[sl, 1], s_cr.at[sl, 1], left),
        ]

    def y_local(t):
        sl = lax.rem(t, 2)
        return pltpu.make_async_copy(ysh.at[sl], out.at[y_rows(t, 0, 0, shard)], s_yl.at[sl])

    def d_copies(t):
        sl = lax.rem(t, 2)
        from_left = y_rows(t, n_chip - 1, 0, hs)
        from_right = y_rows(t, 1, hs, hs)
        return [
            remote(out.at[from_left], out.at[from_left], s_ds.at[sl, 0], s_dr.at[sl, 0], right),
            remote(out.at[from_right], out.at[from_right], s_ds.at[sl, 1], s_dr.at[sl, 1], left),
        ]

    def f_copy(t, group):
        rows = item_rows(t)
        return remote(out.at[rows], out.at[rows], s_f.at[0, group], s_f.at[1, group], mate)

    def phase_a(t):
        for c in a_copies(t):
            c.start()
        xres_load(t)

    def phase_b(t):
        sl = lax.rem(t, 2)

        @pl.when(t >= 2)
        def _():
            for c in b_copies(t - 2):
                c.wait_send()
        first = a_copies(t)
        first[0].wait_recv()
        first[1].wait_recv()
        comb[sl, 0] = (p_v[sh_rows(1, 0, hs), :].astype(F32) + a1r[sl, 0].astype(F32)).astype(BF16)
        comb[sl, 1] = (p_v[sh_rows(n_chip - 1, hs, hs), :].astype(F32) + a1r[sl, 1].astype(F32)).astype(BF16)
        for c in b_copies(t):
            c.start()

    def phase_c(t):
        sl = lax.rem(t, 2)
        a = a_copies(t)
        b = b_copies(t)
        for c in a:
            c.wait_send()
        a[2].wait_recv()
        a[3].wait_recv()
        b[0].wait_recv()
        b[1].wait_recv()
        xres_wait(t)
        for k in range(2):
            rows = pl.ds(k * hs, hs)
            summed = p_v[sh_rows(0, k * hs, hs), :].astype(F32) + br[sl, k].astype(F32) + a2r[sl, 1 - k].astype(F32)
            ysh[sl, rows, :] = (xres[sl, rows, :].astype(F32) + summed.astype(BF16).astype(F32)).astype(BF16)
        for c in c_copies(t):
            c.start()
        y_local(t).start()

    def phase_d(t):
        for c in c_copies(t):
            c.wait_recv()
        y_local(t).wait()
        for c in d_copies(t):
            c.start()

    def phase_e(t):
        for c in d_copies(t):
            c.wait_recv()
            c.wait_send()
        for c in c_copies(t):
            c.wait_send()

        @pl.when((t >= items) & (t < total - late))
        def _():
            f_copy(t, 0).start()

        @pl.when(t >= total - late)
        def _():
            f_copy(t, 1).start()

    lane = lax.broadcasted_iota(jnp.int32, (ROWS, LANES), 1)

    def layer_norm(l):
        xf = x_v[...].astype(F32)
        mean = jnp.mean(xf, axis=-1, keepdims=True)
        centered = xf - mean
        var = jnp.mean(centered * centered, axis=-1, keepdims=True)
        n_v[...] = (centered * lax.rsqrt(var + LN_EPS) * gain[pl.ds(l, 1), :] + bias[pl.ds(l, 1), :]).astype(BF16)

    def qkv(blk, h):
        rows = pl.ds(pl.multiple_of(blk * ROWS, ROWS), ROWS)
        for j in range(heads):
            g = h * heads + j
            y = jnp.dot(n_v[...], wq_v[g], preferred_element_type=F32)
            t0, t1 = y[:, :LANES], y[:, LANES:]
            cs, sn = cos_v[rows, :], sin_v[rows, :]
            for k, v in enumerate((t0 * cs - t1 * sn, t1 * cs + t0 * sn)):
                cols = pl.ds(k * LANES, LANES)
                q_v[g, :, cols] = jnp.where(lane < half_dim, v, 0.0).astype(BF16)
                kv_v[g, rows, cols] = pltpu.roll(v, LANES - half_dim, 1).astype(BF16)

    def attend(g, n):
        scores = lax.dot_general(q_v[g], kv_v[g, :n, :], (((1,), (1,)), ((), ())), preferred_element_type=F32)
        scores = scores * (head_dim ** -0.5 * np.log2(np.e))
        ri = lax.broadcasted_iota(jnp.int32, (ROWS, ROWS), 0)
        ci = lax.broadcasted_iota(jnp.int32, (ROWS, ROWS), 1)
        diag = jnp.where(ri >= ci, scores[:, n - ROWS:], -1e30)
        scores = jnp.concatenate([scores[:, :n - ROWS], diag], axis=1) if n > ROWS else diag
        e = jnp.exp2(scores - jnp.max(scores, axis=1, keepdims=True))
        probs = (e * (1.0 / jnp.sum(e, axis=1, keepdims=True))).astype(BF16)
        return jnp.dot(probs, kv_v[g, :n, :], preferred_element_type=F32)

    def attention(blk, halves):
        for i in range(seq_blocks):
            @pl.when(blk == i)
            def _():
                n = (i + 1) * ROWS

                @pl.loop(0, halves)
                def _(h):
                    base = pl.multiple_of(h * hw, 2 * LANES)
                    acc = [None, None]
                    for j in range(heads):
                        ctx = attend(h * heads + j, n)
                        for k in range(2):
                            c = ctx[:, k * LANES:(k + 1) * LANES]
                            if j == 0:
                                acc[k] = pltpu.roll(c, LANES - half_dim, 1)
                            elif j == 1:
                                acc[k] = jnp.where(lane < half_dim, acc[k], c)
                            elif j == 2:
                                c = pltpu.roll(c, half_dim, 1)
                                v = jnp.where(lane < 2 * half_dim, acc[k], jnp.where(lane < 3 * half_dim, c, 0.0))
                                cu_v[:, pl.ds(base + k * LANES, LANES)] = v.astype(BF16)
                            else:
                                v = jnp.where(lane < half_dim, pltpu.roll(c, LANES - half_dim, 1), 0.0)
                                cu_v[:, pl.ds(base + (2 + k) * LANES, LANES)] = v.astype(BF16)

    def up(h):
        tile = 256
        for n in range(ff // tile):
            y = jnp.dot(n_v[...], wu_v[:, pl.ds(pl.multiple_of(h * ff + n * tile, tile), tile)], preferred_element_type=F32)
            u = 0.5 * y * (1.0 + lax.erf(y * np.float32(0.5 ** 0.5)))
            cu_v[:, pl.ds(pl.multiple_of(h * hw + ow + n * tile, tile), tile)] = u.astype(BF16)

    def down(depth):
        tile = 256
        for n in range(d_model // tile):
            y = jnp.dot(cu_v[:, :depth], wod_v[:depth, n * tile:(n + 1) * tile], preferred_element_type=F32)
            p_v[:, n * tile:(n + 1) * tile] = y.astype(BF16)

    def pm_copy():
        return remote(p_v, pm, s_pm.at[0], s_pm.at[1], mate)

    def f_wait(first, count, group):
        rows = out.at[pl.ds(pl.multiple_of(own_base + first * ROWS, ROWS), count * ROWS)]
        both = remote(rows, rows, s_f.at[0, group], s_f.at[1, group], mate)
        both.wait_send()
        both.wait_recv()

    own_a, mate_a, own_b = final_split(items, late, d_model, 2 * hw)

    def final_load(k):
        def rows(base, first, count):
            return out.at[pl.ds(pl.multiple_of(base + first * ROWS, ROWS), count * ROWS)]

        if k == 0:
            return pltpu.make_async_copy(rows(own_base, 0, own_a), wu_v.at[pl.ds(0, own_a * ROWS)], s_fin.at[0])
        if k == 1:
            return pltpu.make_async_copy(rows(mate_base, 0, mate_a), wod_v.at[pl.ds(0, mate_a * ROWS)], s_fin.at[1])
        return pltpu.make_async_copy(rows(own_base, own_a, own_b), wod_v.at[pl.ds(mate_a * ROWS, own_b * ROWS)], s_fin.at[2])

    barrier = pltpu.get_barrier_semaphore()
    for dev in (left, right, mate):
        pl.semaphore_signal(barrier, inc=1, device_id=dev, device_id_type=MESH)
    x_load(jnp.int32(0))
    for g in range(len(slots)):
        q_copy(0, g).start()
    pl.semaphore_wait(barrier, 3)
    for k in range(2):
        push(0, k).start()

    @pl.loop(0, total + 4)
    def _(i):
        t = i - 1
        tc = jnp.maximum(t, 0)
        compute = i <= total
        blk = lax.rem(tc, seq_blocks)
        halves = jnp.where(i < 2, 1, 2)

        @pl.when((i == 0) | (i == 2))
        def _():
            h = lax.div(i, 2)
            load_q(h)

            @pl.when(i == 0)
            def _():
                for c in own_ud(0):
                    c.start()

            @pl.when(i == 2)
            def _():
                push(0, 1).wait_recv()

            start_o(h)

            @pl.when(i == 2)
            def _():
                qkv(jnp.int32(0), 1)

        @pl.when(compute)
        def _():
            x_wait()
            layer_norm(lax.div(tc, items))

            @pl.when(i < total)
            def _():
                x_load(i + 1)

        @pl.when(t == 1)
        def _():
            phase_b(t - 1)

        @pl.when(t == items)
        def _():
            for c in load_second(0):
                c.wait()

        @pl.when(compute)
        def _():
            @pl.loop(0, halves)
            def _(h):
                qkv(blk, h)

        @pl.when((t >= 2) & (t < total + 1))
        def _():
            phase_b(t - 1)

        @pl.when(t == items - 1)
        def _():
            pq_copy(0).wait()
            po_copy(0).wait()
            for c in load_second(0):
                c.start()

        @pl.when(compute)
        def _():
            attention(blk, halves)

        @pl.when((t >= side_at) & (t < side_at + n_side))
        def _():
            side_job(t - side_at)

        @pl.when((t >= 2) & (t < total + 2))
        def _():
            phase_d(t - 2)

        @pl.when(t >= 3)
        def _():
            phase_e(t - 3)

        @pl.when(compute)
        def _():
            wait_ud(i, 0)

            @pl.loop(0, halves)
            def _(h):
                up(h)

        @pl.when(t == items - 1)
        def _():
            for k in range(2, 4):
                push(1, k).wait_recv()
            for c in load_second(1):
                c.start()

        @pl.when(t == total - 1)
        def _():
            final_load(0).start()

        @pl.when((t >= 1) & (t < total + 1))
        def _():
            phase_c(t - 1)

        @pl.when((i == 0) | (i == 2))
        def _():
            load_o(lax.div(i, 2))

        @pl.when(i < 2)
        def _():
            @pl.when(i == 1)
            def _():
                pm_copy().wait_send()

            wait_ud(i, 1)
            down(hw)

            @pl.when(i == 0)
            def _():
                pm_copy().start()
                for k in range(2, 4):
                    push(0, k).start()

            @pl.when(i == 1)
            def _():
                pm_copy().wait_recv()
                p_v[...] = (p_v[...].astype(F32) + pm[...].astype(F32)).astype(BF16)
                phase_a(t)
                push(0, 0).wait_recv()
                for g in range(len(slots)):
                    q_copy(1, g).start()

        @pl.when((i >= 2) & compute)
        def _():
            wait_ud(i, 1)
            down(2 * hw)
            phase_a(t)

        @pl.when(t == items - 1)
        def _():
            for c in load_second(2):
                c.start()

        @pl.when(t == total - 1)
        def _():
            f_wait(0, mate_a, 0)
            for k in (1, 2):
                final_load(k).start()

        @pl.when(t == 2)
        def _():
            for k in range(4):
                push(1, k).start()

        @pl.when(t == side_at - 1)
        def _():
            side_copy(jnp.int32(0))

    for t in (total - 2, total - 1):
        for c in b_copies(jnp.int32(t)):
            c.wait_send()
    for l in range(layers):
        for i in range(4):
            push(l, i).wait_send()
    f_wait(mate_a, late, 1)
    for k in range(3):
        final_load(k).wait()


def final_split(items, late, rows_a, rows_b):
    own_a = rows_a // ROWS
    mate_a = items - late
    return own_a, mate_a, rows_b // ROWS - mate_a


def collect(cfg, y, va, vb, out, buf, sem):
    items, late = cfg
    core = lax.rem(lax.axis_index("tp"), CORES)
    own_base = core * (items * ROWS)
    mate_base = (CORES - 1 - core) * (items * ROWS)
    own_a, mate_a, own_b = final_split(items, late, va.shape[0], vb.shape[0])

    def rows(base, first, count):
        return pl.ds(pl.multiple_of(base + first * ROWS, ROWS), count * ROWS)

    rest = [(own_base, k) for k in range(own_a + own_b, items)] + [(mate_base, k) for k in range(mate_a, items)]
    ins = [pltpu.make_async_copy(y.at[rows(b, k, 1)], buf.at[n], sem.at[3 + n]) for n, (b, k) in enumerate(rest)]
    outs = [pltpu.make_async_copy(buf.at[n], out.at[rows(b, k, 1)], sem.at[3 + n]) for n, (b, k) in enumerate(rest)]
    direct = [
        pltpu.make_async_copy(va, out.at[rows(own_base, 0, own_a)], sem.at[0]),
        pltpu.make_async_copy(vb.at[pl.ds(0, mate_a * ROWS)], out.at[rows(mate_base, 0, mate_a)], sem.at[1]),
        pltpu.make_async_copy(vb.at[pl.ds(mate_a * ROWS, own_b * ROWS)], out.at[rows(own_base, own_a, own_b)], sem.at[2]),
    ]
    for c in ins + direct:
        c.start()
    for c, d in zip(ins, outs):
        c.wait()
        d.start()
    for c in direct + outs:
        c.wait()


def solution(mesh):
    n_tp = mesh.shape["tp"]
    n_chip = n_tp // CORES

    def shard_body(act_in, ln_gain, ln_bias, w_qkv, w_out, w_up, w_down):
        batch, seq_len, d_model = act_in.shape
        layers, _, heads, group_cols = w_qkv.shape
        head_dim = w_out.shape[1] // heads
        ff = w_up.shape[2]
        assert group_cols == 3 * head_dim and heads == 4 and head_dim == 2 * SLOT
        items = batch * seq_len // (CORES * ROWS)
        blocks = seq_len // ROWS
        late = 4
        cfg = (n_chip, layers, heads, head_dim, d_model, ff, items, blocks, late)
        shard = ROWS // n_chip
        ow = 4 * LANES
        w_q = jnp.transpose(w_qkv, (0, 2, 3, 1))
        cos_tab, sin_tab = rope_tables(seq_len, head_dim)
        vm = pl.BlockSpec(memory_space=pltpu.VMEM)
        hb = pl.BlockSpec(memory_space=pl.ANY)
        dma = pltpu.SemaphoreType.DMA
        out_vmem = (d_model * 2 * ff + (2 * ow + 2 * ff) * d_model) * 2
        res = pl.pallas_call(
            functools.partial(body, cfg),
            name="layers",
            out_shape=[
                jax.ShapeDtypeStruct((batch * seq_len, d_model), BF16),
                pltpu.VMEM((d_model, 2 * ff), BF16),
                pltpu.VMEM((2 * ow + 2 * ff, d_model), BF16),
                jax.ShapeDtypeStruct((layers, heads, group_cols, d_model), BF16),
                jax.ShapeDtypeStruct((layers, heads * head_dim, d_model), BF16),
                jax.ShapeDtypeStruct((d_model, ff), BF16),
                jax.ShapeDtypeStruct((ff, d_model), BF16),
                jax.ShapeDtypeStruct((2 * heads, d_model, 2 * LANES), BF16),
                jax.ShapeDtypeStruct((2 * ow, d_model), BF16),
            ],
            in_specs=[hb] * 5 + [vm] * 5,
            out_specs=[hb, vm, vm] + [hb] * 6,
            scratch_shapes=[
                pltpu.VMEM((2, group_cols, d_model), BF16),
                pltpu.VMEM((d_model, 2 * LANES), BF16),
                pltpu.VMEM((ROWS, d_model), BF16),
                pltpu.VMEM((ROWS, d_model), BF16),
                pltpu.VMEM((ROWS, d_model), BF16),
                pltpu.VMEM((2 * heads, ROWS, 2 * LANES), BF16),
                pltpu.VMEM((2 * heads, seq_len, 2 * LANES), BF16),
                pltpu.VMEM((ROWS, 2 * ow + 2 * ff), BF16),
                pltpu.VMEM((ROWS, d_model), BF16),
                pltpu.VMEM((2 * heads, d_model, 2 * LANES), BF16),
                pltpu.VMEM((2, 2, shard // 2, d_model), BF16),
                pltpu.VMEM((2, 2, shard // 2, d_model), BF16),
                pltpu.VMEM((2, 2, shard // 2, d_model), BF16),
                pltpu.VMEM((2, 2, shard // 2, d_model), BF16),
                pltpu.VMEM((2, shard, d_model), BF16),
                pltpu.VMEM((2, shard, d_model), BF16),
                dma((2, 2)), dma((2, 2)), dma((2, 2)), dma((2, 2)), dma((2, 2)), dma((2, 2)),
                dma((2, 2)), dma((2, 2)), dma((2, 2)), dma((2, 2)),
                dma((2,)), dma, dma((2,)), dma((2, 2)), dma((2, 2)), dma((2, 4)), dma((2, 4)), dma((3,)), dma((2,)),
                dma((2,)), dma((3,)), dma((3,)),
            ],
            compiler_params=pltpu.CompilerParams(collective_id=0, has_side_effects=True, vmem_limit_bytes=VMEM_LIMIT - out_vmem),
        )(act_in.reshape(batch * seq_len, d_model), w_q, w_out, w_up, w_down, ln_gain, ln_bias, jnp.asarray(cos_tab), jnp.asarray(sin_tab), jnp.asarray(regroup(head_dim), BF16))
        own_a, mate_a, own_b = final_split(items, late, d_model, 2 * ow + 2 * ff)
        rest = 2 * items - own_a - mate_a - own_b
        y = pl.pallas_call(
            functools.partial(collect, (items, late)),
            name="collect",
            out_shape=jax.ShapeDtypeStruct((batch * seq_len, d_model), BF16),
            in_specs=[hb, vm, vm],
            out_specs=hb,
            scratch_shapes=[pltpu.VMEM((rest, ROWS, d_model), BF16), dma((3 + rest,))],
            compiler_params=pltpu.CompilerParams(vmem_limit_bytes=16 << 20),
        )(*res[:3])
        return y.reshape(batch, seq_len, d_model)

    return jax.shard_map(shard_body, mesh=mesh, in_specs=(P("dp", None, None), P(None, None), P(None, None), P(None, None, "tp", None), P(None, "tp", None), P(None, None, "tp"), P(None, "tp", None)), out_specs=P("dp", None, None), check_vma=False)
```

time: 805 us -> 736 us (0.914)
  local copies, waits for them, and re-layouts: 63.3 us -> 0 us
    unnamed x1 -> x0, local copies, waits for them, and re-layouts: 29 us -> none
    pallas_call x1, Pallas kernels: 738 us -> 719 us  [shard_body(): pl.pallas_call(functools.partial(body, cfg), name='layers', out_shape=[ja...]
    pallas_call x0 -> x1, Pallas kernels: none -> 16.8 us  [shard_body(): pl.pallas_call(functools.partial(collect, (items, late)), name='collect',...]
    reshape x1 -> x0, local copies, waits for them, and re-layouts: 13.8 us -> none  [prep_qkv(): return w.reshape(layers, heads, d_model, 2 * LANES)]
    transpose x3 -> x0, local copies, waits for them, and re-layouts: 10.5 us -> none  [the longest x1 8.41 us: prep_qkv(): jnp.transpose(w, (0, 2, 1, 4, 3, 5))]
    pad x1 -> x0, local copies, waits for them, and re-layouts: 8.95 us -> none  [prep_qkv(): w = jnp.pad(w, ((0, 0),) * 4 + ((0, LANES - 3 * half_dim),))]
where the time goes in v2:
time: 736 us; the launch traced here: 735 us
  Pallas kernels  735 us (100%)
    pallas_call x1, Pallas kernels, shard_body(): pl.pallas_call(functools.partial(body, cfg), name='layers', out_shape=[ja...  719 us
    pallas_call x1, Pallas kernels, shard_body(): pl.pallas_call(functools.partial(collect, (items, late)), name='collect',...  16.8 us

profile of v2, /device:TPU:113, one launch (start us, length us, event | category | flops | bytes accessed | tf_op | source)
XLA Modules:
  0.0 735.4 jit_solution(1214063060155803613)
XLA Ops:
  0.0 718.6 %layers.1 = (bf16[8192,2560]{1,0:T(8,128)(2,1)}, bf16[2560,2560]{1,0:T(8,128)(2,1)S(1)}, bf16[3584,2560]{1,0:T(8,128)(2,1)S(1)}, bf16[2,4,240,2560]{3,2,1,0:T(8,...) custom-call(bf16[8192,2560]{1,0:T(8,128)(2,1)} %bitcast.3, ...), custom_call_target="tpu_custom_call" | custom-call | tf_op jit(solution)/shard_map/layers/pallas_call | solution.py:702
  718.6 16.8 %collect.1 = bf16[8192,2560]{1,0:T(8,128)(2,1)} custom-call(bf16[8192,2560]{1,0:T(8,128)(2,1)} %get-tuple-element.8.y, bf16[2560,2560]{1,0:T(8,128)(2,1)S(1)} %get-tuple-element.9.va, bf16[3584,2560]{1,0:T(8,128)(2,1)S(1)} %get-tuple-element.10.vb), custom_call_target="tpu_custom_call" | custom-call | tf_op jit(solution)/shard_map/collect/pallas_call | solution.py:744

commit v3 on v0

v3 whole, which is shorter than its diff:
```python
import functools

import jax
import jax.numpy as jnp
import numpy as np
from jax import lax
from jax.experimental import pallas as pl
from jax.experimental.pallas import tpu as pltpu
from jax.sharding import PartitionSpec as P

LN_EPS = 1e-5
ROPE_BASE = 10000.0
F32 = jnp.float32
BF16 = jnp.bfloat16
MESH = pl.DeviceIdType.MESH
VMEM_LIMIT = 67043328

CORES = 2
ROWS = 256
LANES = 128
SLOT = 40
LN_ROWS = 128
UNROLLED = 3


def rope_tables(seq_len, head_dim):
    half_dim = head_dim // 2
    inv_freq = (ROPE_BASE ** (-2.0 * np.arange(half_dim, dtype=np.float32) / head_dim)).astype(np.float32)
    angles = np.arange(seq_len, dtype=np.float32)[:, None] * inv_freq[None, :]
    cos_tab = np.ones((seq_len, LANES), np.float32)
    sin_tab = np.zeros((seq_len, LANES), np.float32)
    for k in range(2):
        cos_tab[:, k * half_dim:(k + 1) * half_dim] = np.cos(angles)
        sin_tab[:, k * half_dim:(k + 1) * half_dim] = np.sin(angles)
    return np.concatenate([cos_tab, sin_tab], axis=1)


def regroup(head_dim):
    half_dim = head_dim // 2
    sel = np.zeros((3 * head_dim, 2 * LANES), np.float32)
    for part in range(3):
        for half in range(2):
            for i in range(half_dim):
                sel[(part * 2 + half) * half_dim + i, half * LANES + part * half_dim + i] = 1.0
    return sel


def body(cfg, act, w_q, w_o, w_u, w_d, gain, bias, tab, sel_v,
         out, wu_v, wod_v, st_q, st_o, st_u, st_d, pq, po,
         tab_v, pst, pm, x_v, n_v, q_v, kv_v, cu_v, p_v, wq_v,
         ar, br, ysh, br2, ysh2,
         s_as, s_ar, s_ar2, s_bs, s_br, s_br2, s_cs, s_cr, s_co, s_ds, s_do, s_y1, s_yl, s_x, s_xr, s_f, s_wl, s_ws, s_wr, s_m2s, s_m2r,
         s_gs, s_gx, s_gp, s_stg, s_pm, s_pq, s_rl, s_fin, s_tab, s_kv, s_ca, s_cb, s_rdy):
    n_chip, layers, heads, head_dim, d_model, ff, items, blocks, late = cfg
    side_at = 9
    group_cols = 3 * head_dim
    seq_blocks = blocks
    group_cols = 3 * head_dim
    half_dim = head_dim // 2
    total = layers * items
    tp = lax.axis_index("tp")
    dp = lax.axis_index("dp")
    chip = lax.div(tp, CORES)
    core = lax.rem(tp, CORES)
    twin = lax.rem(dp, 2)
    odd = lax.rem(chip, 2)
    pair = lax.div(chip, 2)
    inn = chip + 1 - 2 * odd
    outn = lax.rem(chip + n_chip - 1 + 2 * odd, n_chip)

    def dev(c, k):
        return {"tp": c * CORES + k}

    inn_d, outn_d, mate = dev(inn, core), dev(outn, core), dev(chip, CORES - 1 - core)
    peer = {"dp": dp + 1 - 2 * twin, "tp": tp}
    own_base = core * (items * ROWS)
    mate_base = (CORES - 1 - core) * (items * ROWS)
    half = ROWS // 2
    quart = ROWS // 4
    ow = 4 * LANES
    hw = ow + ff

    def remote(src, dst, ssem, rsem, dev):
        return pltpu.make_async_remote_copy(src_ref=src, dst_ref=dst, send_sem=ssem, recv_sem=rsem, device_id=dev, device_id_type=MESH)

    def at(base, off, size):
        return pl.ds(pl.multiple_of(base + off, quart), size)

    def rows1(t, off, size):
        return at(own_base + lax.rem(t, items) * ROWS, off, size)

    def rows2(t, p, off, size):
        u = t - items
        q = lax.div(u, blocks)
        cc = lax.rem(q, CORES)
        seq = p + cc - 2 * p * cc + 2 * lax.div(q, CORES)
        return at(cc * (items * ROWS) + (seq * blocks + lax.rem(u, blocks)) * ROWS, off, size)

    def owner(t):
        return lax.rem(lax.div(t, blocks) + core, 2) == pair

    def ud_dst(h):
        return [wu_v.at[:, pl.ds(h * ff, ff)], wod_v.at[pl.ds(h * hw + ow, ff)]]

    def own_ud(l):
        return [pltpu.make_async_copy(s.at[l], d, s_wl.at[0, i]) for i, (s, d) in enumerate(zip((w_u, w_d), ud_dst(0)))]

    def staged_ud(h):
        return [pltpu.make_async_copy(s.at[h], d, s_wl.at[h, i]) for i, (s, d) in enumerate(zip((st_u, st_d), ud_dst(h)))]

    def push(i):
        src = (wq_v.at[pl.ds(0, heads)], wod_v.at[pl.ds(0, ow)], w_u.at[0], w_d.at[0])[i]
        dst = (wq_v.at[pl.ds(heads, heads)], wod_v.at[pl.ds(hw, ow)], *ud_dst(1))[i]
        return remote(src, dst, s_ws.at[i], s_wr.at[i], mate)

    def push_kv():
        rows = pl.ds(0, ROWS)
        return remote(kv_v.at[pl.ds(0, heads), rows], kv_v.at[pl.ds(heads, heads), rows], s_kv.at[0], s_kv.at[1], mate)

    args2 = (w_q.at[1], w_o.at[1], w_u.at[1], w_d.at[1])
    staged = (st_q, st_o, st_u, st_d)

    def push2(i):
        return remote(args2[i], staged[i].at[1], s_m2s.at[i], s_m2r.at[i], mate)

    pieces = []
    for k, (n_rows, step) in enumerate(((heads * group_cols, quart), (heads * head_dim, quart), (d_model, 2 * quart), (ff, quart))):
        pieces += [(k, r, step) for r in range(0, n_rows, step)]
    groups = [pieces[j:j + 4] for j in range(0, len(pieces), 4)]

    def group_send(j, k):
        arr, r, n = groups[j][k]
        rows = pl.ds(r, n)
        return remote(args2[arr].at[rows], staged[arr].at[twin, rows], s_gs.at[0], s_gx.at[j], dev(outn, 1))

    def group_pass(j):
        copies = []
        for arr in range(4):
            mine = [p for p in groups[j] if p[0] == arr]
            if mine:
                rows = pl.ds(mine[0][1], sum(p[2] for p in mine))
                copies.append(remote(staged[arr].at[twin, rows], staged[arr].at[twin, rows], s_gs.at[1], s_gp.at[j], peer))
        return copies

    def group_bytes(j, sem, n=1):
        rows = out.at[pl.ds(0, n * ROWS)]
        return remote(rows, rows, s_gs.at[j], sem, peer)

    def regroup_q(src, dst, unroll=False):
        def one(c):
            part = pl.ds(c, 512) if unroll else pl.ds(pl.multiple_of(c, 512), 512)
            y = lax.dot_general(src[:, part], sel_v[...], (((0,), (0,)), ((), ())), preferred_element_type=F32)
            dst[part, :] = y.astype(BF16)

        if unroll:
            for c in range(0, d_model, 512):
                one(c)
        else:
            pl.loop(0, d_model, step=512)(one)

    def regroup_o(src, dst):
        @pl.loop(0, d_model, step=512)
        def _(c):
            part = pl.ds(pl.multiple_of(c, 512), 512)
            y = lax.dot_general(sel_v[...], src[:, part], (((0,), (0,)), ((), ())), preferred_element_type=F32)
            dst[:, part] = y.astype(BF16)

    slots = (p_v.at[1, pl.ds(0, group_cols)], p_v.at[2, pl.ds(0, group_cols)], cu_v.at[pl.ds(0, group_cols), pl.ds(0, d_model)])

    def q_copy(g):
        return pltpu.make_async_copy(w_q.at[0, pl.ds(g * group_cols, group_cols)], slots[g % len(slots)], s_stg.at[g % len(slots)])

    def load_q():
        for g in range(heads):
            q_copy(g).wait()
            regroup_q(slots[g % len(slots)], wq_v.at[g])
            if g + len(slots) < heads:
                q_copy(g + len(slots)).start()

    def o_copy(src, k, dst):
        rows = (pl.ds(0, group_cols), pl.ds(group_cols, head_dim))[k]
        return pltpu.make_async_copy(src.at[rows], dst.at[pl.ds(0, (group_cols, head_dim)[k])], s_stg.at[k])

    def clear_tail(ref):
        ref[pl.ds(head_dim, group_cols - head_dim), :] = jnp.zeros((group_cols - head_dim, d_model), BF16)

    def load_o():
        for k in range(2):
            o_copy(w_o.at[0], k, slots[k]).wait()
            regroup_o(slots[k], wod_v.at[pl.ds(k * 2 * LANES, 2 * LANES)])

    n_side = 2 * heads + 4
    side_refs = (n_v.at[pl.ds(0, group_cols)], slots[2])

    def side_copy(a, k):
        for h in range(2):
            for arg in range(2 - h):
                from_arg = (core == 0) if arg else ((core == 1) if h == 0 else (core >= 0))

                @pl.when((a >= h * heads) & (a < (h + 1) * heads) & from_arg)
                def _():
                    rows = pl.ds(pl.multiple_of((a - h * heads) * group_cols, group_cols), group_cols)
                    src = w_q.at[1, rows] if arg else st_q.at[h, rows]
                    pltpu.make_async_copy(src, side_refs[k], s_stg.at[k]).start()

                @pl.when((a == 2 * heads + 2 * h + k) & from_arg)
                def _():
                    if k:
                        clear_tail(side_refs[k])
                    o_copy(w_o.at[1] if arg else st_o.at[h], k, side_refs[k]).start()

    def pq_copy(g):
        return pltpu.make_async_copy(pst, pq.at[g], s_pq.at[0])

    def po_copy(b):
        return pltpu.make_async_copy(pm, po.at[pl.ds(pl.multiple_of(b * 2 * LANES, 2 * LANES), 2 * LANES)], s_pq.at[1])

    def side_job(a, k):
        @pl.when(a < 2 * heads)
        def _():
            pltpu.make_async_copy(w_q.at[1, pl.ds(0, group_cols)], side_refs[k], s_stg.at[k]).wait()

            @pl.when(a > 0)
            def _():
                pq_copy(a - 1).wait()

            regroup_q(side_refs[k], pst)
            pq_copy(a).start()

        @pl.when(a >= 2 * heads)
        def _():
            o_copy(w_o.at[1], k, side_refs[k]).wait()

            @pl.when(a > 2 * heads)
            def _():
                po_copy(a - 2 * heads - 1).wait()

            regroup_o(side_refs[k], pm)
            po_copy(a - 2 * heads).start()

    def start_second(k):
        if k == 0:
            second(0)[0].start()
            return

        @pl.when(core == 0)
        def _():
            own_ud(1)[k - 1].start()

        @pl.when(core == 1)
        def _():
            staged_ud(0)[k - 1].start()

        for c in second(k)[1:]:
            c.start()

    def second(k):
        if k == 0:
            return [pltpu.make_async_copy(pq, wq_v, s_rl.at[0])]
        outs = [pltpu.make_async_copy(po.at[pl.ds(h * ow, ow)], wod_v.at[pl.ds(h * hw, ow)], s_rl.at[1 + h]) for h in range(2)]
        return [staged_ud(h)[k - 1] for h in range(2)] + (outs if k == 2 else [])

    def wait_ud(i, k):
        @pl.when(i == 0)
        def _():
            own_ud(0)[k].wait()

        @pl.when(i == 2)
        def _():
            push(2 + k).wait_recv()

        @pl.when(i == items + 1)
        def _():
            for c in second(1 + k):
                c.wait()

    def weights_here(first, last, mate_pieces):
        @pl.when(core == 0)
        def _():
            for k in mate_pieces:
                push2(k).wait_recv()

        @pl.when(core == 1)
        def _():
            for j in range(first, last):
                group_bytes(0, s_gp.at[j]).wait_recv()

    def x_load(i):
        t = i - 1

        @pl.when(i == 0)
        def _():
            pltpu.make_async_copy(act.at[pl.ds(pl.multiple_of(mate_base, ROWS), ROWS)], x_v, s_x).start()

        @pl.when((i >= 1) & (t < items))
        def _():
            pltpu.make_async_copy(act.at[rows1(t, 0, ROWS)], x_v, s_x).start()

        @pl.when(t >= items)
        def _():
            q = lax.div(t - items, blocks)

            @pl.when((lax.rem(t, blocks) == 0) & (lax.rem(q, CORES) != core))
            def _():
                seq = out.at[pl.ds(0, blocks * ROWS)]
                remote(seq, seq, s_y1.at[0], s_y1.at[1 + lax.div(q, CORES)], mate).wait_recv()

            pltpu.make_async_copy(out.at[rows2(t, pair, 0, ROWS)], x_v, s_x).start()

    def x_wait():
        pltpu.make_async_copy(act.at[pl.ds(0, ROWS)], x_v, s_x).wait()

    def sl(t):
        return lax.rem(t, 2)

    def s3(t):
        return lax.rem(t, 3)

    def nth(t):
        return lax.div(t, 2 * blocks) * blocks + lax.rem(t, blocks)

    def prow(t, off, size):
        return (s3(t), at(0, off, size))

    def a1(t):
        off = jnp.where(owner(t), 1 - odd, odd) * half
        return remote(p_v.at[prow(t, off, half)], ar.at[s3(t)], s_as.at[s3(t)], s_ar.at[s3(t)], inn_d)

    def b1(t):
        return remote(ar.at[s3(t)], br, s_bs.at[0], s_br.at[0], outn_d)

    def c1(t):
        rows = rows1(t, odd * half, half)
        return [
            remote(ysh, out.at[rows], s_cs.at[0, 0], s_cr.at[0, lax.rem(t, 4)], inn_d),
            remote(ysh, out.at[rows], s_cs.at[0, 1], s_y1.at[1 + lax.div(t, 2 * blocks)], mate),
        ]

    def l1(t):
        return pltpu.make_async_copy(ysh, out.at[rows1(t, odd * half, half)], s_yl.at[0])

    def d1(t):
        rows = rows1(t, (1 - odd) * half, half)
        return remote(out.at[rows], out.at[rows], s_ds.at[0, sl(t)], s_y1.at[1 + lax.div(t, 2 * blocks)], mate)

    def r1(t):
        return pltpu.make_async_copy(act.at[rows1(t, odd * half, half)], ysh, s_xr.at[0])

    def a2(t):
        return remote(p_v.at[prow(t, (1 - core) * half, half)], pm.at[at(0, sl(t) * half, half)], s_as.at[3], s_ar2.at[sl(t)], mate)

    def b2(t):
        return remote(pm.at[at(0, sl(t) * half + (1 - odd) * quart, quart)], br2.at[sl(t)], s_bs.at[1], s_br2.at[sl(t)], inn_d)

    def c2(t):
        rows = rows2(t, pair, core * half + odd * quart, quart)
        return [
            remote(ysh2, out.at[rows], s_cs.at[1, 0], s_cr.at[1, lax.rem(t, 4)], inn_d),
            remote(ysh2, out.at[rows], s_cs.at[1, 1], s_co.at[lax.rem(t, 4)], outn_d),
        ]

    def l2(t):
        return pltpu.make_async_copy(ysh2, out.at[rows2(t, pair, core * half + odd * quart, quart)], s_yl.at[1])

    def d2(t):
        rows = rows2(t, pair, core * half + (1 - odd) * quart, quart)
        return remote(out.at[rows], out.at[rows], s_ds.at[1, sl(t)], s_do.at[lax.rem(t, 4)], outn_d)

    def r2(t):
        return pltpu.make_async_copy(out.at[rows2(t, pair, core * half + odd * quart, quart)], ysh2, s_xr.at[1])

    def f2(t, group):
        copies = []
        for p in (pair, 1 - pair):
            rows = rows2(t, p, core * half, half)
            copies.append(remote(out.at[rows], out.at[rows], s_f.at[0, group], s_f.at[1, group], mate))
        return copies

    def f32(x):
        return x.astype(F32)

    def by_rows(n, f):
        @pl.loop(0, n // 16)
        def _(i):
            f(lambda base=0: pl.ds(pl.multiple_of(base + i * 16, 16), 16))

    def slot_free(t):
        @pl.when(t + 3 < items)
        def _():
            pl.semaphore_signal(s_ca, inc=1, device_id=inn_d, device_id_type=MESH)

    def phase_a(t):
        @pl.when(t < items)
        def _():
            @pl.when(t >= 3)
            def _():
                pl.semaphore_wait(s_ca, 1)

            a1(t).start()

            @pl.when((t == 0) & owner(t))
            def _():
                r1(t).start()

        @pl.when(t >= items)
        def _():
            @pl.when(t == items)
            def _():
                pl.semaphore_wait(s_rdy, 1)

            a2(t).start()

            @pl.when(t == items)
            def _():
                r2(t).start()

    def phase_b1(t):
        @pl.when(jnp.logical_not(owner(t)))
        def _():
            n = nth(t)

            @pl.when(n > 0)
            def _():
                pl.semaphore_wait(s_cb, 1)

            a1(t).wait_recv()
            k = s3(t)

            def add(rows):
                ar[k, rows(), :] = (f32(p_v[k, rows((1 - odd) * half), :]) + f32(ar[k, rows(), :])).astype(BF16)

            by_rows(half, add)
            b1(t).start()

    def phase_c1(t):
        a1(t).wait_send()

        @pl.when(jnp.logical_not(owner(t)))
        def _():
            b1(t).wait_send()
            slot_free(t)

        @pl.when(owner(t))
        def _():
            a1(t).wait_recv()
            b1(t).wait_recv()
            r1(t).wait()
            k = s3(t)

            def add(rows):
                summed = f32(p_v[k, rows(odd * half), :]) + f32(ar[k, rows(), :]) + f32(br[rows(), :])
                ysh[rows(), :] = (f32(ysh[rows(), :]) + f32(summed.astype(BF16))).astype(BF16)

            by_rows(half, add)
            slot_free(t)

            @pl.when(nth(t) + 1 < items // 2)
            def _():
                pl.semaphore_signal(s_cb, inc=1, device_id=outn_d, device_id_type=MESH)

            for c in c1(t):
                c.start()
            l1(t).start()

    def phase_d1(t):
        @pl.when(owner(t))
        def _():
            c1(t)[0].wait_recv()
            l1(t).wait()
            for c in c1(t):
                c.wait_send()
            d1(t).start()

        @pl.when((t + 1 < items) & owner(t + 1))
        def _():
            r1(t + 1).start()

    def phase_e1(t):
        @pl.when(owner(t))
        def _():
            d1(t).wait_send()

    def phase_b2(t):
        a2(t).wait_recv()
        k, m = s3(t), sl(t) * half

        def add(rows):
            pm[rows(m + (1 - odd) * quart), :] = (f32(p_v[k, rows(core * half + (1 - odd) * quart), :]) + f32(pm[rows(m + (1 - odd) * quart), :])).astype(BF16)

        by_rows(quart, add)
        b2(t).start()

    def phase_c2(t):
        a2(t).wait_send()
        b2(t).wait_recv()
        r2(t).wait()
        k, k2, m = s3(t), sl(t), sl(t) * half

        def add(rows):
            summed = f32(p_v[k, rows(core * half + odd * quart), :]) + f32(pm[rows(m + odd * quart), :]) + f32(br2[k2, rows(), :])
            ysh2[rows(), :] = (f32(ysh2[rows(), :]) + f32(summed.astype(BF16))).astype(BF16)

        by_rows(quart, add)
        for c in c2(t):
            c.start()
        l2(t).start()
        b2(t).wait_send()

    def phase_d2(t):
        c2(t)[0].wait_recv()
        l2(t).wait()
        for c in c2(t):
            c.wait_send()
        d2(t).start()

        @pl.when(t + 1 < total)
        def _():
            r2(t + 1).start()

    def phase_e2(t):
        d2(t).wait_send()
        c2(t)[1].wait_recv()
        d2(t).wait_recv()

        @pl.when(t < total - late)
        def _():
            for c in f2(t, 0):
                c.start()

        @pl.when(t >= total - late)
        def _():
            for c in f2(t, 1):
                c.start()

    def lagged(phase, t, layer):
        lo, hi = layer * items, (layer + 1) * items

        @pl.when((t >= lo) & (t < hi))
        def _():
            phase(t)

    lane = lax.broadcasted_iota(jnp.int32, (ROWS, LANES), 1)

    def layer_norm(l):
        step = LN_ROWS

        @pl.loop(0, ROWS // step)
        def _(i):
            r = pl.ds(pl.multiple_of(i * step, step), step)
            xf = x_v[r, :].astype(F32)
            mean = jnp.mean(xf, axis=-1, keepdims=True)
            centered = xf - mean
            var = jnp.mean(centered * centered, axis=-1, keepdims=True)
            n_v[r, :] = (centered * lax.rsqrt(var + LN_EPS) * gain[pl.ds(l, 1), :] + bias[pl.ds(l, 1), :]).astype(BF16)

    def tab_copy(blk):
        return pltpu.make_async_copy(tab.at[pl.ds(pl.multiple_of(blk * ROWS, ROWS), ROWS)], tab_v, s_tab)

    def qkv(blk, g):
        rows = pl.ds(pl.multiple_of(blk * ROWS, ROWS), ROWS)
        y = jnp.dot(n_v[...], wq_v[g], preferred_element_type=F32)
        t0, t1 = y[:, :LANES], y[:, LANES:]
        cs, sn = tab_v[:, :LANES], tab_v[:, LANES:]
        for k, v in enumerate((t0 * cs - t1 * sn, t1 * cs + t0 * sn)):
            cols = pl.ds(k * LANES, LANES)
            q_v[g, :, cols] = jnp.where(lane < half_dim, v, 0.0).astype(BF16)
            kv_v[g, rows, cols] = pltpu.roll(v, LANES - half_dim, 1).astype(BF16)

    def qkv_half():
        @pl.loop(0, heads, step=2)
        def _(g):
            for j in range(2):
                qkv(jnp.int32(0), g + j)

    def attend(g, n):
        scores = lax.dot_general(q_v[g], kv_v[g, :n, :], (((1,), (1,)), ((), ())), preferred_element_type=F32)
        ri = lax.broadcasted_iota(jnp.int32, (ROWS, ROWS), 0)
        ci = lax.broadcasted_iota(jnp.int32, (ROWS, ROWS), 1)
        diag = jnp.where(ri >= ci, scores[:, n - ROWS:], -1e30)
        scores = jnp.concatenate([scores[:, :n - ROWS], diag], axis=1) if n > ROWS else diag
        e = jnp.exp2((scores - jnp.max(scores, axis=1, keepdims=True)) * np.float32(head_dim ** -0.5 * np.log2(np.e)))
        probs = (e * (1.0 / jnp.sum(e, axis=1, keepdims=True))).astype(BF16)
        return jnp.dot(probs, kv_v[g, :n, :], preferred_element_type=F32)

    def four_heads(h, n):
        base = h * hw
        ctx = [attend(h * heads + j, n) for j in range(heads)]
        for k in range(2):
            first, second, third, fourth = (c[:, k * LANES:(k + 1) * LANES] for c in ctx)
            v = jnp.where(lane < half_dim, pltpu.roll(first, LANES - half_dim, 1), second)
            w = jnp.where(lane < 3 * half_dim, pltpu.roll(third, half_dim, 1), 0.0)
            cu_v[:, pl.ds(pl.multiple_of(base + k * LANES, LANES), LANES)] = jnp.where(lane < 2 * half_dim, v, w).astype(BF16)
            v = jnp.where(lane < half_dim, pltpu.roll(fourth, LANES - half_dim, 1), 0.0)
            cu_v[:, pl.ds(pl.multiple_of(base + (2 + k) * LANES, LANES), LANES)] = v.astype(BF16)

    def attention(blk):
        for i in range(blocks):
            @pl.when(blk == i)
            def _():
                if i < UNROLLED:
                    for h in range(2):
                        four_heads(h, (i + 1) * ROWS)
                else:
                    pl.loop(0, 2)(lambda h: four_heads(h, (i + 1) * ROWS))

    tile = 2 * LANES

    def cols(n):
        return pl.ds(pl.multiple_of(n * tile, tile), tile)

    def up(h, n):
        y = jnp.dot(n_v[...], wu_v[:, cols(h * (ff // tile) + n)], preferred_element_type=F32)
        u = 0.5 * y * (1.0 + lax.erf(y * np.float32(0.5 ** 0.5)))
        cu_v[:, cols((h * hw + ow) // tile + n)] = u.astype(BF16)

    def down(depth, slot, n):
        y = jnp.dot(cu_v[:, :depth], wod_v[:depth, cols(n)], preferred_element_type=F32)
        p_v[slot, :, cols(n)] = y.astype(BF16)

    def pm_copy():
        return remote(p_v.at[0], pm, s_pm.at[0], s_pm.at[1], mate)

    def f_wait(count, group):
        rows = out.at[pl.ds(0, count * ROWS)]
        both = remote(rows, rows, s_f.at[0, group], s_f.at[1, group], mate)
        both.wait_send()
        both.wait_recv()

    in_u, in_od = d_model, 2 * hw

    def final_load(k):
        if k == 0:
            return pltpu.make_async_copy(out.at[pl.ds(0, in_u)], wu_v, s_fin.at[0])
        return pltpu.make_async_copy(out.at[pl.ds(in_u, in_od)], wod_v, s_fin.at[1])

    def send_group(i, k):
        for j in range(2, len(groups)):
            @pl.when((i == j) & (core == twin))
            def _():
                group_send(j, k).start()

    barrier = pltpu.get_barrier_semaphore()
    for d in (inn_d, outn_d, mate, dev(outn, CORES - 1 - core), peer):
        pl.semaphore_signal(barrier, inc=1, device_id=d, device_id_type=MESH)
    x_load(jnp.int32(0))
    tab_copy(jnp.int32(0)).start()
    for g in range(len(slots)):
        q_copy(g).start()
    pl.semaphore_wait(barrier, 5)

    @pl.when(core == twin)
    def _():
        for j in range(2):
            for k in range(4):
                group_send(j, k).start()

    @pl.loop(0, total + 4)
    def _(i):
        t = i - 1
        tc = jnp.maximum(t, 0)
        compute = i <= total
        small = i < 2
        whole = (i >= 2) & compute
        blk = lax.rem(tc, blocks)
        job = (t - side_at) * 2
        has_jobs = (t >= side_at) & (t < side_at + n_side // 2)

        def on(cond):
            return pl.when(cond)

        @on(i == 0)
        def _():
            load_q()
            clear_tail(slots[1])
            for k in range(2):
                o_copy(w_o.at[0], k, slots[k]).start()
            for c in own_ud(0):
                c.start()

        @on(compute)
        def _():
            x_wait()
            layer_norm(lax.div(tc, items))

            @on(i < total)
            def _():
                x_load(i + 1)

        @on(i == 0)
        def _():
            push(0).start()

        send_group(i, 0)
        for j in range(len(groups)):
            @on((t == j + 1) & (core == 1))
            def _():
                group_bytes(1, s_gx.at[j]).wait_recv()
                for c in group_pass(j):
                    c.start()

        @on(t == items)
        def _():
            for c in second(0):
                c.wait()

        @on(i == 1)
        def _():
            push_kv().wait_send()

        @on(i == 2)
        def _():
            push(0).wait_recv()
            push_kv().wait_recv()

        @on(compute & (i != 1))
        def _():
            tab_copy(blk).wait()

        @on(small)
        def _():
            qkv_half()

        @on(whole)
        def _():
            for g in range(2 * heads):
                qkv(blk, g)

        @on((i >= 1) & (i < total))
        def _():
            tab_copy(lax.rem(i, blocks)).start()

        lagged(phase_b2, t - 1, 1)

        @on((t > side_at) & (t <= side_at + n_side // 2))
        def _():
            side_job(job - 1, 1)

        @on(t == items - 1)
        def _():
            pq_copy(0).wait()
            po_copy(0).wait()
            pl.semaphore_signal(s_rdy, inc=1, device_id=mate, device_id_type=MESH)
            start_second(0)

        send_group(i, 1)

        @on(small)
        def _():
            four_heads(0, ROWS)

        @on(i == 0)
        def _():
            push_kv().start()

        @on(whole)
        def _():
            attention(blk)

        send_group(i, 2)

        @on(compute)
        def _():
            wait_ud(i, 0)

            @on(small)
            def _():
                pl.loop(0, ff // tile)(lambda n: up(0, n))

            @on(whole)
            def _():
                for h in range(2):
                    for n in range(ff // tile):
                        up(h, n)

        @on(has_jobs)
        def _():
            side_copy(job, 0)

        @on(t == items - 1)
        def _():
            weights_here(5, 10, (2,))
            start_second(1)

        @on(t == total - 1)
        def _():
            f_wait(items - late, 0)
            final_load(0).start()

        lagged(phase_e1, t - 5, 0)
        lagged(phase_e2, t - 3, 1)
        lagged(phase_d1, t - 4, 0)
        lagged(phase_d2, t - 2, 1)
        lagged(phase_c1, t - 3, 0)
        lagged(phase_b1, t - 2, 0)
        send_group(i, 3)

        @on(small)
        def _():
            @on(i == 0)
            def _():
                load_o()

            @on(i == 1)
            def _():
                pm_copy().wait_send()

            wait_ud(i, 1)

            @pl.loop(0, d_model // tile, step=2)
            def _(n):
                for k in range(2):
                    down(hw, 0, n + k)

            @on(i == 0)
            def _():
                pm_copy().start()
                for k in range(1, 4):
                    push(k).start()

            @on(i == 1)
            def _():
                pm_copy().wait_recv()

                def add(rows):
                    p_v[0, rows(), :] = (f32(p_v[0, rows(), :]) + f32(pm[rows(), :])).astype(BF16)

                by_rows(ROWS, add)

        @on(i == 2)
        def _():
            push(1).wait_recv()

        @on(whole)
        def _():
            wait_ud(i, 1)
            for n in range(d_model // tile):
                down(2 * hw, s3(t), n)

        lagged(phase_c2, t - 1, 1)

        @on((i >= 1) & compute)
        def _():
            phase_a(t)

        @on(has_jobs)
        def _():
            side_copy(job + 1, 1)
            side_job(job, 0)

        @on(t == items - 1)
        def _():
            weights_here(10, len(groups), (3,))
            start_second(2)

        @on(t == total - 1)
        def _():
            final_load(1).start()

        @on(t == 2)
        def _():
            for k in range(4):
                push(k).wait_send()

            @on(core == 1)
            def _():
                for k in range(4):
                    push2(k).start()

        @on(t == side_at - 1)
        def _():
            weights_here(0, 5, (0, 1))


    @pl.when(core == 1)
    def _():
        for i in range(4):
            push2(i).wait_send()
        group_bytes(1, s_gx.at[0], len(groups)).wait_send()

    @pl.when(core == twin)
    def _():
        group_bytes(0, s_gx.at[0], len(groups)).wait_send()

    f_wait(late, 1)
    for k in range(2):
        final_load(k).wait()


def collect(y, va, vb, out, buf, sem):
    na, nb = va.shape[0], vb.shape[0]
    spans = [pl.ds(na + nb + n * ROWS, ROWS) for n in range(buf.shape[0])]
    ins = [pltpu.make_async_copy(y.at[r], buf.at[n], sem.at[2 + n]) for n, r in enumerate(spans)]
    outs = [pltpu.make_async_copy(buf.at[n], out.at[r], sem.at[2 + n]) for n, r in enumerate(spans)]
    direct = [
        pltpu.make_async_copy(va, out.at[pl.ds(0, na)], sem.at[0]),
        pltpu.make_async_copy(vb, out.at[pl.ds(na, nb)], sem.at[1]),
    ]
    for c in ins + direct:
        c.start()
    for c, d in zip(ins, outs):
        c.wait()
        d.start()
    for c in direct + outs:
        c.wait()


def solution(mesh):
    n_tp = mesh.shape["tp"]
    n_chip = n_tp // CORES

    def shard_body(act_in, ln_gain, ln_bias, w_qkv, w_out, w_up, w_down):
        batch, seq_len, d_model = act_in.shape
        layers, _, heads, group_cols = w_qkv.shape
        head_dim = w_out.shape[1] // heads
        ff = w_up.shape[2]
        assert group_cols == 3 * head_dim and heads == 4 and head_dim == 2 * SLOT
        items = batch * seq_len // (CORES * ROWS)
        blocks = seq_len // ROWS
        late = 4
        cfg = (n_chip, layers, heads, head_dim, d_model, ff, items, blocks, late)
        ow = 4 * LANES
        quart = ROWS // 4
        n_groups = (heads * group_cols + heads * head_dim + d_model // 2 + ff) // ROWS
        w_q = jnp.transpose(w_qkv, (0, 2, 3, 1)).reshape(layers, heads * group_cols, d_model)
        vm = pl.BlockSpec(memory_space=pltpu.VMEM)
        hb = pl.BlockSpec(memory_space=pl.ANY)
        dma = pltpu.SemaphoreType.DMA
        two, three, four, square, many = (dma(n) for n in ((2,), (3,), (4,), (2, 2), (n_groups,)))
        plain = pltpu.SemaphoreType.REGULAR
        out_vmem = (d_model * 2 * ff + (2 * ow + 2 * ff) * d_model) * 2
        res = pl.pallas_call(
            functools.partial(body, cfg),
            name="layers",
            out_shape=[
                jax.ShapeDtypeStruct((batch * seq_len, d_model), BF16),
                pltpu.VMEM((d_model, 2 * ff), BF16),
                pltpu.VMEM((2 * ow + 2 * ff, d_model), BF16),
                jax.ShapeDtypeStruct((2, heads * group_cols, d_model), BF16),
                jax.ShapeDtypeStruct((2, heads * head_dim, d_model), BF16),
                jax.ShapeDtypeStruct((2, d_model, ff), BF16),
                jax.ShapeDtypeStruct((2, ff, d_model), BF16),
                jax.ShapeDtypeStruct((2 * heads, d_model, 2 * LANES), BF16),
                jax.ShapeDtypeStruct((2 * ow, d_model), BF16),
            ],
            in_specs=[hb] * 5 + [vm] * 2 + [hb, vm],
            out_specs=[hb, vm, vm] + [hb] * 6,
            scratch_shapes=[
                pltpu.VMEM((ROWS, 2 * LANES), F32),
                pltpu.VMEM((d_model, 2 * LANES), BF16),
                pltpu.VMEM((ROWS, d_model), BF16),
                pltpu.VMEM((ROWS, d_model), BF16),
                pltpu.VMEM((ROWS, d_model), BF16),
                pltpu.VMEM((2 * heads, ROWS, 2 * LANES), BF16),
                pltpu.VMEM((2 * heads, seq_len, 2 * LANES), BF16),
                pltpu.VMEM((ROWS, 2 * ow + 2 * ff), BF16),
                pltpu.VMEM((3, ROWS, d_model), BF16),
                pltpu.VMEM((2 * heads, d_model, 2 * LANES), BF16),
                pltpu.VMEM((3, 2 * quart, d_model), BF16),
                pltpu.VMEM((2 * quart, d_model), BF16),
                pltpu.VMEM((2 * quart, d_model), BF16),
                pltpu.VMEM((2, quart, d_model), BF16),
                pltpu.VMEM((quart, d_model), BF16),
                four, three, two, two, two, two, square, dma((layers, 4)), four, square, four, three, two,
                dma, two, square, square, four, four, four, four,
                two, many, many, three, two, two, three, two,
                dma, two, plain, plain, plain,
            ],
            compiler_params=pltpu.CompilerParams(collective_id=0, has_side_effects=True, vmem_limit_bytes=VMEM_LIMIT - out_vmem),
        )(act_in.reshape(batch * seq_len, d_model), w_q, w_out, w_up, w_down, ln_gain, ln_bias, jnp.asarray(rope_tables(seq_len, head_dim)), jnp.asarray(regroup(head_dim), BF16))
        rest = batch * seq_len // ROWS - (d_model + 2 * ow + 2 * ff) // ROWS
        y = pl.pallas_call(
            collect,
            name="collect",
            out_shape=jax.ShapeDtypeStruct((batch * seq_len, d_model), BF16),
            in_specs=[hb, vm, vm],
            out_specs=hb,
            scratch_shapes=[pltpu.VMEM((rest, ROWS, d_model), BF16), dma((2 + rest,))],
            compiler_params=pltpu.CompilerParams(vmem_limit_bytes=16 << 20),
        )(*res[:3])
        return y.reshape(batch, seq_len, d_model)

    wide = P(None, None, "tp")
    tall = P(None, "tp")
    return jax.shard_map(shard_body, mesh=mesh, in_specs=(P("dp"), P(), P(), wide, tall, wide, tall), out_specs=P("dp"), check_vma=False)
```

time: 1950 us -> 668 us (0.34)
  matrix products: 828 us -> 0 us
  waiting for transfers between devices: 825 us -> 0 us
  Pallas kernels: 0 us -> 668 us
  other arithmetic: 249 us -> 0 us
  local copies, waits for them, and re-layouts: 28.4 us -> 0 us
    dot_general x12 -> x0, matrix products: 828 us -> none  [the longest x2 306 us: layer_partial(): jnp.einsum('bsf,fe->bse', gelu_out, w_down, preferred_element_type=jnp.fl...]
    psum x2 -> x0, waiting for transfers between devices: 825 us -> none  [shard_body(): reduced = lax.psum(local_sum, 'tp')]
    pallas_call x0 -> x2, Pallas kernels: none -> 668 us  [the longest x1 651 us: shard_body(): pl.pallas_call(functools.partial(body, cfg), name='layers', out_shape=[ja...]
    reduce_sum x6 -> x0, other arithmetic: 175 us -> none  [the longest x2 82.6 us: layer_partial(): attn_probs = jax.nn.softmax(scores, axis=-1).astype(jnp.bfloat16)]
    convert_element_type x1 -> x0, other arithmetic: 41.3 us -> none  [shard_body(): (hidden.astype(jnp.float32) + reduced.astype(jnp.float32)).astype(jnp.bfl...]
    concatenate x3 -> x0, other arithmetic: 20.9 us -> none  [apply_rope(): jnp.concatenate([first * cos_tab - second * sin_tab, second * cos_tab + f...]
  transfers between devices with their start and end apart: 2 -> 0, of which waited for: 2 -> 0; matrix products, arithmetic and copies ran while one was open for 0% -> 0% of each run, Pallas kernels for 0% -> 0%
where the time goes in v3:
time: 668 us
  Pallas kernels  668 us (100%)
    pallas_call x1, Pallas kernels, shard_body(): pl.pallas_call(functools.partial(body, cfg), name='layers', out_shape=[ja...  651 us
    pallas_call x1, Pallas kernels, shard_body(): pl.pallas_call(collect, name='collect', out_shape=jax.ShapeDtypeStruct((b...  16.8 us

profile of v3, /device:TPU:113, one launch (start us, length us, event | category | flops | bytes accessed | tf_op | source)
XLA Modules:
  0.0 668.1 jit_solution(17122792620483447980)
XLA Ops:
  0.0 651.2 %layers.1 = (bf16[8192,2560]{1,0:T(8,128)(2,1)}, bf16[2560,2560]{1,0:T(8,128)(2,1)S(1)}, bf16[3584,2560]{1,0:T(8,128)(2,1)S(1)}, bf16[2,960,2560]{2,1,0:T(8,128)...) custom-call(bf16[8192,2560]{1,0:T(8,128)(2,1)} %bitcast.5, ...), custom_call_target="tpu_custom_call" | custom-call | tf_op jit(solution)/shard_map/layers/pallas_call | solution.py:931
  651.2 16.8 %collect.1 = bf16[8192,2560]{1,0:T(8,128)(2,1)} custom-call(bf16[8192,2560]{1,0:T(8,128)(2,1)} %get-tuple-element.8.y, bf16[2560,2560]{1,0:T(8,128)(2,1)S(1)} %get-tuple-element.9.va, bf16[3584,2560]{1,0:T(8,128)(2,1)S(1)} %get-tuple-element.10.vb), custom_call_target="tpu_custom_call" | custom-call | tf_op jit(solution)/shard_map/collect/pallas_call | solution.py:971

commit v4 on v3

--- a/solution.py
+++ b/solution.py
@@ -49,7 +49,7 @@
          out, wu_v, wod_v, st_q, st_o, st_u, st_d, pq, po,
          tab_v, pst, pm, x_v, n_v, q_v, kv_v, cu_v, p_v, wq_v,
          ar, br, ysh, br2, ysh2,
-         s_as, s_ar, s_ar2, s_bs, s_br, s_br2, s_cs, s_cr, s_co, s_ds, s_do, s_y1, s_yl, s_x, s_xr, s_f, s_wl, s_ws, s_wr, s_m2s, s_m2r,
+         s_as, s_ar, s_ar2, s_bs, s_br, s_br2, s_cs, s_cr, s_cr2, s_co, s_ds, s_do, s_y1, s_yl, s_x, s_xr, s_f, s_wl, s_ws, s_wr, s_m2s, s_m2r,
          s_gs, s_gx, s_gp, s_stg, s_pm, s_pq, s_rl, s_fin, s_tab, s_kv, s_ca, s_cb, s_rdy):
     n_chip, layers, heads, head_dim, d_model, ff, items, blocks, late = cfg
     side_at = 9
@@ -84,7 +84,7 @@
         return pltpu.make_async_remote_copy(src_ref=src, dst_ref=dst, send_sem=ssem, recv_sem=rsem, device_id=dev, device_id_type=MESH)
 
     def at(base, off, size):
-        return pl.ds(pl.multiple_of(base + off, quart), size)
+        return pl.ds(pl.multiple_of(base + off, min(size, quart)), size)
 
     def rows1(t, off, size):
         return at(own_base + lax.rem(t, items) * ROWS, off, size)
@@ -158,24 +158,37 @@
         else:
             pl.loop(0, d_model, step=512)(one)
 
-    def regroup_o(src, dst):
-        @pl.loop(0, d_model, step=512)
-        def _(c):
-            part = pl.ds(pl.multiple_of(c, 512), 512)
+    def regroup_o(src, dst, unroll=False):
+        def one(c):
+            part = pl.ds(c, 512) if unroll else pl.ds(pl.multiple_of(c, 512), 512)
             y = lax.dot_general(sel_v[...], src[:, part], (((0,), (0,)), ((), ())), preferred_element_type=F32)
             dst[:, part] = y.astype(BF16)
 
-    slots = (p_v.at[1, pl.ds(0, group_cols)], p_v.at[2, pl.ds(0, group_cols)], cu_v.at[pl.ds(0, group_cols), pl.ds(0, d_model)])
+        if unroll:
+            for c in range(0, d_model, 512):
+                one(c)
+        else:
+            pl.loop(0, d_model, step=512)(one)
+
+    def slot(k):
+        return p_v.at[k, pl.ds(0, group_cols)]
+
+    n_slots = 3
 
     def q_copy(g):
-        return pltpu.make_async_copy(w_q.at[0, pl.ds(g * group_cols, group_cols)], slots[g % len(slots)], s_stg.at[g % len(slots)])
+        rows = pl.ds(pl.multiple_of(g * group_cols, group_cols), group_cols)
+        k = lax.rem(g, n_slots)
+        return pltpu.make_async_copy(w_q.at[0, rows], slot(k), s_stg.at[k])
 
     def load_q():
-        for g in range(heads):
+        @pl.loop(0, heads)
+        def _(g):
             q_copy(g).wait()
-            regroup_q(slots[g % len(slots)], wq_v.at[g])
-            if g + len(slots) < heads:
-                q_copy(g + len(slots)).start()
+            regroup_q(slot(lax.rem(g, n_slots)), wq_v.at[g], True)
+
+            @pl.when(g + n_slots < heads)
+            def _():
+                q_copy(g + n_slots).start()
 
     def o_copy(src, k, dst):
         rows = (pl.ds(0, group_cols), pl.ds(group_cols, head_dim))[k]
@@ -186,11 +199,14 @@
 
     def load_o():
         for k in range(2):
-            o_copy(w_o.at[0], k, slots[k]).wait()
-            regroup_o(slots[k], wod_v.at[pl.ds(k * 2 * LANES, 2 * LANES)])
+            o_copy(w_o.at[0], k, slot(k)).wait()
+
+        @pl.loop(0, 2)
+        def _(k):
+            regroup_o(slot(k), wod_v.at[pl.ds(pl.multiple_of(k * 2 * LANES, 2 * LANES), 2 * LANES)], True)
 
     n_side = 2 * heads + 4
-    side_refs = (n_v.at[pl.ds(0, group_cols)], slots[2])
+    side_refs = (n_v.at[pl.ds(0, group_cols)], cu_v.at[pl.ds(0, group_cols), pl.ds(0, d_model)])
 
     def side_copy(a, k):
         for h in range(2):
@@ -332,7 +348,7 @@
     def c1(t):
         rows = rows1(t, odd * half, half)
         return [
-            remote(ysh, out.at[rows], s_cs.at[0, 0], s_cr.at[0, lax.rem(t, 4)], inn_d),
+            remote(ysh, out.at[rows], s_cs.at[0, 0], s_cr.at[lax.rem(t, 4)], inn_d),
             remote(ysh, out.at[rows], s_cs.at[0, 1], s_y1.at[1 + lax.div(t, 2 * blocks)], mate),
         ]
 
@@ -349,22 +365,34 @@
     def a2(t):
         return remote(p_v.at[prow(t, (1 - core) * half, half)], pm.at[at(0, sl(t) * half, half)], s_as.at[3], s_ar2.at[sl(t)], mate)
 
-    def b2(t):
-        return remote(pm.at[at(0, sl(t) * half + (1 - odd) * quart, quart)], br2.at[sl(t)], s_bs.at[1], s_br2.at[sl(t)], inn_d)
-
-    def c2(t):
-        rows = rows2(t, pair, core * half + odd * quart, quart)
+    piece = quart // 2
+
+    def b2(t, p):
+        m = sl(t) * half + (1 - odd) * quart
+        dst = br2.at[sl(t), pl.ds(p * piece, piece)]
+        return remote(pm.at[piece_rows(m, p)], dst, s_bs.at[1], s_br2.at[sl(t), p], inn_d)
+
+    def piece_rows(base, p):
+        return pl.ds(pl.multiple_of(base + p * piece, piece), piece)
+
+    def c2(t, p):
+        rows = rows2(t, pair, core * half + odd * quart + p * piece, piece)
+        src = ysh2.at[pl.ds(p * piece, piece)]
+        k = lax.rem(t, 4)
         return [
-            remote(ysh2, out.at[rows], s_cs.at[1, 0], s_cr.at[1, lax.rem(t, 4)], inn_d),
-            remote(ysh2, out.at[rows], s_cs.at[1, 1], s_co.at[lax.rem(t, 4)], outn_d),
+            remote(src, out.at[rows], s_cs.at[1, 0], s_cr2.at[k, p], inn_d),
+            remote(src, out.at[rows], s_cs.at[1, 1], s_co.at[k, p], outn_d),
         ]
 
     def l2(t):
         return pltpu.make_async_copy(ysh2, out.at[rows2(t, pair, core * half + odd * quart, quart)], s_yl.at[1])
 
-    def d2(t):
-        rows = rows2(t, pair, core * half + (1 - odd) * quart, quart)
-        return remote(out.at[rows], out.at[rows], s_ds.at[1, sl(t)], s_do.at[lax.rem(t, 4)], outn_d)
+    def d2(t, p):
+        rows = rows2(t, pair, core * half + (1 - odd) * quart + p * piece, piece)
+        return remote(out.at[rows], out.at[rows], s_ds.at[1, sl(t)], s_do.at[lax.rem(t, 4), p], outn_d)
+
+    def sent2(sem):
+        return remote(ysh2, ysh2, sem, s_cr2.at[0, 0], inn_d).wait_send()
 
     def r2(t):
         return pltpu.make_async_copy(out.at[rows2(t, pair, core * half + odd * quart, quart)], ysh2, s_xr.at[1])
@@ -483,44 +511,51 @@
     def phase_b2(t):
         a2(t).wait_recv()
         k, m = s3(t), sl(t) * half
-
-        def add(rows):
-            pm[rows(m + (1 - odd) * quart), :] = (f32(p_v[k, rows(core * half + (1 - odd) * quart), :]) + f32(pm[rows(m + (1 - odd) * quart), :])).astype(BF16)
-
-        by_rows(quart, add)
-        b2(t).start()
+        for p in range(2):
+            q = (1 - odd) * quart + p * piece
+
+            def add(rows):
+                pm[rows(m + q), :] = (f32(p_v[k, rows(core * half + q), :]) + f32(pm[rows(m + q), :])).astype(BF16)
+
+            by_rows(piece, add)
+            b2(t, p).start()
 
     def phase_c2(t):
         a2(t).wait_send()
-        b2(t).wait_recv()
         r2(t).wait()
         k, k2, m = s3(t), sl(t), sl(t) * half
-
-        def add(rows):
-            summed = f32(p_v[k, rows(core * half + odd * quart), :]) + f32(pm[rows(m + odd * quart), :]) + f32(br2[k2, rows(), :])
-            ysh2[rows(), :] = (f32(ysh2[rows(), :]) + f32(summed.astype(BF16))).astype(BF16)
-
-        by_rows(quart, add)
-        for c in c2(t):
-            c.start()
+        for p in range(2):
+            q = odd * quart + p * piece
+            o = p * piece
+
+            def add(rows):
+                summed = f32(p_v[k, rows(core * half + q), :]) + f32(pm[rows(m + q), :]) + f32(br2[k2, rows(o), :])
+                ysh2[rows(o), :] = (f32(ysh2[rows(o), :]) + f32(summed.astype(BF16))).astype(BF16)
+
+            b2(t, p).wait_recv()
+            by_rows(piece, add)
+            for c in c2(t, p):
+                c.start()
         l2(t).start()
-        b2(t).wait_send()
+        sent2(s_bs.at[1])
 
     def phase_d2(t):
-        c2(t)[0].wait_recv()
+        for p in range(2):
+            c2(t, p)[0].wait_recv()
+            d2(t, p).start()
         l2(t).wait()
-        for c in c2(t):
-            c.wait_send()
-        d2(t).start()
+        for k in range(2):
+            sent2(s_cs.at[1, k])
 
         @pl.when(t + 1 < total)
         def _():
             r2(t + 1).start()
 
     def phase_e2(t):
-        d2(t).wait_send()
-        c2(t)[1].wait_recv()
-        d2(t).wait_recv()
+        sent2(s_ds.at[1, sl(t)])
+        for p in range(2):
+            c2(t, p)[1].wait_recv()
+            d2(t, p).wait_recv()
 
         @pl.when(t < total - late)
         def _():
@@ -567,10 +602,8 @@
             kv_v[g, rows, cols] = pltpu.roll(v, LANES - half_dim, 1).astype(BF16)
 
     def qkv_half():
-        @pl.loop(0, heads, step=2)
-        def _(g):
-            for j in range(2):
-                qkv(jnp.int32(0), g + j)
+        for g in range(heads):
+            qkv(jnp.int32(0), g)
 
     def attend(g, n):
         scores = lax.dot_general(q_v[g], kv_v[g, :n, :], (((1,), (1,)), ((), ())), preferred_element_type=F32)
@@ -644,8 +677,8 @@
         pl.semaphore_signal(barrier, inc=1, device_id=d, device_id_type=MESH)
     x_load(jnp.int32(0))
     tab_copy(jnp.int32(0)).start()
-    for g in range(len(slots)):
-        q_copy(g).start()
+    for g in range(n_slots):
+        q_copy(jnp.int32(g)).start()
     pl.semaphore_wait(barrier, 5)
 
     @pl.when(core == twin)
@@ -671,9 +704,9 @@
         @on(i == 0)
         def _():
             load_q()
-            clear_tail(slots[1])
+            clear_tail(slot(1))
             for k in range(2):
-                o_copy(w_o.at[0], k, slots[k]).start()
+                o_copy(w_o.at[0], k, slot(k)).start()
             for c in own_ud(0):
                 c.start()
 
@@ -764,7 +797,8 @@
 
             @on(small)
             def _():
-                pl.loop(0, ff // tile)(lambda n: up(0, n))
+                for n in range(ff // tile):
+                    up(0, n)
 
             @on(whole)
             def _():
@@ -925,7 +959,7 @@
         vm = pl.BlockSpec(memory_space=pltpu.VMEM)
         hb = pl.BlockSpec(memory_space=pl.ANY)
         dma = pltpu.SemaphoreType.DMA
-        two, three, four, square, many = (dma(n) for n in ((2,), (3,), (4,), (2, 2), (n_groups,)))
+        two, three, four, square, pieces4, many = (dma(n) for n in ((2,), (3,), (4,), (2, 2), (4, 2), (n_groups,)))
         plain = pltpu.SemaphoreType.REGULAR
         out_vmem = (d_model * 2 * ff + (2 * ow + 2 * ff) * d_model) * 2
         res = pl.pallas_call(
@@ -960,7 +994,7 @@
                 pltpu.VMEM((2 * quart, d_model), BF16),
                 pltpu.VMEM((2, quart, d_model), BF16),
                 pltpu.VMEM((quart, d_model), BF16),
-                four, three, two, two, two, two, square, dma((layers, 4)), four, square, four, three, two,
+                four, three, two, two, two, square, square, four, pieces4, pieces4, square, pieces4, three, two,
                 dma, two, square, square, four, four, four, four,
                 two, many, many, three, two, two, three, two,
                 dma, two, plain, plain, plain,

time: 668 us -> 663 us (level)
  no operation moved by 1% of the time
where the time goes in v4:
time: 663 us
  Pallas kernels  663 us (100%)
    pallas_call x1, Pallas kernels, shard_body(): pl.pallas_call(functools.partial(body, cfg), name='layers', out_shape=[ja...  646 us
    pallas_call x1, Pallas kernels, shard_body(): pl.pallas_call(collect, name='collect', out_shape=jax.ShapeDtypeStruct((b...  16.8 us

profile of v4, /device:TPU:113, one launch (start us, length us, event | category | flops | bytes accessed | tf_op | source)
XLA Modules:
  0.0 662.9 jit_solution(9952043860255524087)
XLA Ops:
  0.0 646.1 %layers.1 = (bf16[8192,2560]{1,0:T(8,128)(2,1)}, bf16[2560,2560]{1,0:T(8,128)(2,1)S(1)}, bf16[3584,2560]{1,0:T(8,128)(2,1)S(1)}, bf16[2,960,2560]{2,1,0:T(8,128)...) custom-call(bf16[8192,2560]{1,0:T(8,128)(2,1)} %bitcast.5, ...), custom_call_target="tpu_custom_call" | custom-call | tf_op jit(solution)/shard_map/layers/pallas_call | solution.py:965
  646.1 16.8 %collect.1 = bf16[8192,2560]{1,0:T(8,128)(2,1)} custom-call(bf16[8192,2560]{1,0:T(8,128)(2,1)} %get-tuple-element.8.y, bf16[2560,2560]{1,0:T(8,128)(2,1)S(1)} %get-tuple-element.9.va, bf16[3584,2560]{1,0:T(8,128)(2,1)S(1)} %get-tuple-element.10.vb), custom_call_target="tpu_custom_call" | custom-call | tf_op jit(solution)/shard_map/collect/pallas_call | solution.py:1005

commit v5 on v4

--- a/solution.py
+++ b/solution.py
@@ -20,7 +20,7 @@
 LANES = 128
 SLOT = 40
 LN_ROWS = 128
-UNROLLED = 3
+UNROLLED = 4
 
 
 def rope_tables(seq_len, head_dim):

time: 663 us -> 662 us (level)
  no operation moved by 1% of the time
where the time goes in v5:
time: 662 us
  Pallas kernels  662 us (100%)
    pallas_call x1, Pallas kernels, shard_body(): pl.pallas_call(functools.partial(body, cfg), name='layers', out_shape=[ja...  645 us
    pallas_call x1, Pallas kernels, shard_body(): pl.pallas_call(collect, name='collect', out_shape=jax.ShapeDtypeStruct((b...  16.8 us

profile of v5, /device:TPU:113, one launch (start us, length us, event | category | flops | bytes accessed | tf_op | source)
XLA Modules:
  0.0 661.9 jit_solution(11085069057589381083)
XLA Ops:
  0.0 645.0 %layers.1 = (bf16[8192,2560]{1,0:T(8,128)(2,1)}, bf16[2560,2560]{1,0:T(8,128)(2,1)S(1)}, bf16[3584,2560]{1,0:T(8,128)(2,1)S(1)}, bf16[2,960,2560]{2,1,0:T(8,128)...) custom-call(bf16[8192,2560]{1,0:T(8,128)(2,1)} %bitcast.5, ...), custom_call_target="tpu_custom_call" | custom-call | tf_op jit(solution)/shard_map/layers/pallas_call | solution.py:965
  645.0 16.8 %collect.1 = bf16[8192,2560]{1,0:T(8,128)(2,1)} custom-call(bf16[8192,2560]{1,0:T(8,128)(2,1)} %get-tuple-element.8.y, bf16[2560,2560]{1,0:T(8,128)(2,1)S(1)} %get-tuple-element.9.va, bf16[3584,2560]{1,0:T(8,128)(2,1)S(1)} %get-tuple-element.10.vb), custom_call_target="tpu_custom_call" | custom-call | tf_op jit(solution)/shard_map/collect/pallas_call | solution.py:1005
